TPU v7x, 256 devices: a whole 4x4x8 slice. The times are simulated.
256 devices in a mesh: rep: 4 (over y), shard: 64 (over x, z, core).
Axes of the slice: x: 4, y: 4, z: 8, core: 2. Of those that a mesh axis runs over, the one named last changes fastest.
Arguments:
- item_ids: int32 [512, 1024], P(('rep', 'shard')), may hold values from 0 to 524287, as said below
- seq_lengths: int32 [4, 128], P('rep'), may hold values from 64 to 1024, as said below
- seq_owner: int32 [4, 128], P('rep'), may hold values from 0 to 63, as said below
- row_home: int32 [524288], replicated, may hold values from 0 to 524287, as said below
- item_table: bfloat16 [524288, 256], P('shard', 'rep'), may hold values from -6 to 6
- proj_weight: bfloat16 [256, 1024], replicated, may hold values from -0.375 to 0.375
- out_weight: bfloat16 [256, 256], replicated, may hold values from -0.375 to 0.375
Outputs:
- mixed: bfloat16 [512, 1024, 256], P(('rep', 'shard'))
Inputs may be any that keep to these rules, and one draw needn't show every extreme that they name: `item_ids`: for every history and every shard index k, at most 32 of its 1024 slots name items with row_home[item] // 8192 == k; in every draw one shard index is named by exactly 32 slots of every history. `row_home`: A permutation of the table rows. `seq_lengths`: each group has a history of exactly 1024 live events. `seq_owner`: every shard index owns exactly 2 histories of each group.
All inputs are finite; a program needn't handle non-finite values.
Results may differ from a plain program's by a relative error of at most 0.0058.
Values may be sent and summed in bfloat16 or wider, within the bound.
A program may use at most 64 MiB of HBM per device.

v0:
```python
import math

import jax
import jax.numpy as jnp
from jax import lax
from jax.sharding import PartitionSpec as P

HEADS = 4


EPSILON = 1e-06


def joined_along(blocks, dim):
    blocks = jnp.moveaxis(blocks, 0, dim)
    shape = blocks.shape
    return blocks.reshape(*shape[:dim], shape[dim] * shape[dim + 1], *shape[dim + 2 :])


def from_everyone(array, axis):
    size = lax.axis_size(axis)
    return lax.all_to_all(
        jnp.broadcast_to(array[None], (size, *array.shape)), axis, 0, 0, tiled=True
    )


def gathered_copies(array, axis, dim):
    return joined_along(from_everyone(array, axis), dim)


def layer_norm(values):
    center = values - jnp.mean(values, axis=-1, keepdims=True)
    spread = jnp.mean(center * center, axis=-1, keepdims=True)
    return center * lax.rsqrt(spread + EPSILON)


def head_norm(values):
    center = values - jnp.mean(values, axis=(0, 2), keepdims=True)
    spread = jnp.mean(center * center, axis=(0, 2), keepdims=True)
    return center * lax.rsqrt(spread + EPSILON)


def bucket_ranks(target, groups):
    onehot = (target[:, None] == jnp.arange(groups, dtype=jnp.int32)[None, :]).astype(jnp.int32)
    running = jnp.cumsum(onehot, axis=0) - onehot
    return jnp.sum(running * onehot, axis=1)


def block_terms(query, keys, values, q_start, k_start, length, scale):
    scores = jnp.einsum("hqd,hkd->hqk", query, keys, preferred_element_type=jnp.float32) * scale
    rows = q_start + jnp.arange(query.shape[1], dtype=jnp.int32)
    cols = k_start + jnp.arange(keys.shape[1], dtype=jnp.int32)
    keep = cols[None, :] <= rows[:, None]
    weights = jnp.where(keep[None], jax.nn.silu(scores) / length.astype(jnp.float32), 0.0).astype(
        jnp.bfloat16
    )
    return jnp.einsum("hqk,hkd->hqd", weights, values, preferred_element_type=jnp.float32)


def body(item_ids, seq_lengths, seq_owner, row_home, item_table, proj_weight, out_weight):
    shards = lax.axis_size("shard")
    me = lax.axis_index("shard")
    seq_dev, seq_len = item_ids.shape
    width = proj_weight.shape[0]
    head_dim = width // HEADS
    events = seq_dev * seq_len
    owners = seq_owner[0]
    lengths = seq_lengths[0]
    order = jnp.argsort(owners, stable=True)
    mine = lax.dynamic_slice_in_dim(order, me * seq_dev, seq_dev)
    my_lengths = lengths[mine]
    table = lax.all_gather(item_table, "rep", axis=1, tiled=True)
    rows_dev = table.shape[0]
    capacity = seq_dev * (2 * seq_len // shards)
    histories = gathered_copies(item_ids, "shard", 0)
    my_ids = jnp.take(histories, mine, axis=0).reshape(events)
    home = row_home[my_ids]
    target = home // rows_dev
    slot = target * capacity + bucket_ranks(target, shards)
    asked = jnp.zeros((shards * capacity,), jnp.int32).at[slot].set(home % rows_dev)
    fetched = lax.all_to_all(
        jnp.take(
            table,
            lax.all_to_all(
                asked.reshape(shards, capacity), "shard", split_axis=0, concat_axis=0, tiled=True
            ),
            axis=0,
        ),
        "shard",
        split_axis=0,
        concat_axis=0,
        tiled=True,
    )
    embedded = jnp.take(fetched.reshape(shards * capacity, width), slot, axis=0)
    normed = layer_norm(embedded.astype(jnp.float32)).astype(jnp.bfloat16)
    weight_heads = proj_weight.reshape(width, 4, HEADS, head_dim)
    proj = jax.nn.silu(
        jnp.einsum("ed,dchf->chef", normed, weight_heads, preferred_element_type=jnp.float32)
    ).astype(jnp.bfloat16)
    gate = proj[0]
    values = proj[1].reshape(HEADS, seq_dev, seq_len, head_dim)
    queries = proj[2].reshape(HEADS, seq_dev, seq_len, head_dim)
    keys = proj[3].reshape(HEADS, seq_dev, seq_len, head_dim)
    block = min(512, seq_len)
    blocks = seq_len // block
    scale = 1.0 / math.sqrt(head_dim)
    results = []
    for seq in range(seq_dev):
        length = my_lengths[seq]
        seq_keys = keys[:, seq]
        seq_values = values[:, seq]
        pieces = []
        for qb in range(blocks):
            query = queries[:, seq, qb * block : (qb + 1) * block]
            empty = jnp.zeros((HEADS, block, head_dim), jnp.float32)
            needed = jnp.where(
                qb * block < length, jnp.minimum(qb + 1, (length + block - 1) // block), 0
            )

            def add_block(
                kb,
                total,
                query=query,
                seq_keys=seq_keys,
                seq_values=seq_values,
                length=length,
                qb=qb,
            ):
                key_block = lax.dynamic_slice_in_dim(seq_keys, kb * block, block, 1)
                value_block = lax.dynamic_slice_in_dim(seq_values, kb * block, block, 1)
                return total + block_terms(
                    query, key_block, value_block, qb * block, kb * block, length, scale
                )

            total = lax.fori_loop(0, needed, add_block, empty)
            pieces.append(total)
        results.append(jnp.concatenate(pieces, axis=1))
    attended = jnp.stack(results, axis=1).reshape(HEADS, events, head_dim)
    gated = (head_norm(attended) * gate.astype(jnp.float32)).astype(jnp.bfloat16)
    out_heads = out_weight.reshape(HEADS, head_dim, width)
    mixed = embedded.astype(jnp.float32) + jnp.einsum(
        "hef,hfo->eo", gated, out_heads, preferred_element_type=jnp.float32
    )
    places = jnp.arange(seq_len, dtype=jnp.int32)
    live = (places[None, :] < my_lengths[:, None]).reshape(events, 1)
    return jnp.where(live, mixed, 0.0).astype(jnp.bfloat16).reshape(seq_dev, seq_len, width)


def solution(mesh):
    in_specs = (
        P(("rep", "shard"), None),
        P("rep", None),
        P("rep", None),
        P(),
        P("shard", "rep"),
        P(),
        P(),
    )
    out_specs = P(("rep", "shard"), None, None)
    return jax.shard_map(body, mesh=mesh, in_specs=in_specs, out_specs=out_specs, check_vma=False)
```

profile of v0, /device:TPU:1, one launch (start us, length us, event | category | flops | bytes accessed | tf_op | source)
XLA Modules:
  0.0 246.9 jit_solution(6338347634809303210)
XLA Ops:
  8.9 13.0 %all-to-all-start = ((s32[64,2,1024]{2,1,0:T(2,128)}), s32[64,2,1024]{2,1,0:T(2,128)S(1)}, u32[]{:S(2)}, u32[]{:S(2)}) async-start(s32[64,2,1024]{2,1,0:T(2,128)} %broadcast_in_dim.135), calls=%async_computation | async-start | bytes 1048576 | tf_op jit(solution)/shard_map/all_to_all | solution.py:22
  21.9 3.3 %sort.17 = (s32[128]{0:T(128)}, s32[128]{0:T(128)S(1)}) sort(s32[128]{0:T(128)} %bitcast.252, s32[128]{0:T(128)S(1)} %iota.76), dimensions={0}, to_apply=%region_0.0 | sort | flops 896 | bytes 2048 | tf_op jit(solution)/shard_map/jit(argsort)/sort | solution.py:69
  25.2 13.9 %all-to-all-done = s32[64,2,1024]{2,1,0:T(2,128)S(1)} async-done(((s32[64,2,1024]{2,1,0:T(2,128)}), s32[64,2,1024]{2,1,0:T(2,128)S(1)}, u32[]{:S(2)}, u32[]{:S(2)}) %all-to-all-start) | async-done | bytes 524320 | tf_op jit(solution)/shard_map/all_to_all | solution.py:22
  40.2 11.8 %gather_fusion.2 = s32[2048]{0:T(1024)S(1)} fusion(s32[524288]{0:T(1024)S(1)} %copy-done, s32[2048]{0:T(1024)S(1)} %broadcast_clamp_fusion.2), kind=kCustom, calls=%fused_computation.2 | custom fusion | bytes 24576 | tf_op jit(solution)/shard_map/gather | solution.py:77
  52.1 18.1 %reduce-window.6 = s32[64,16,128]{2,1,0:T(8,128)S(1)} reduce-window(s32[64,16,128]{2,1,0:T(8,128)S(1)} %fusion.83, s32[]{:T(128)} %constant.241.clone.1), window={size=1x1x128 pad=0_0x0_0x127_0}, to_apply=%region_1.2 | reduce-window | flops 16646144 | bytes 1048580 | tf_op jit(solution)/shard_map/reduce-window
  71.6 8.1 %scatter_custom_fusion = s32[4096]{0:T(1024)S(1)} fusion(s32[2048]{0:T(1024)S(1)} %bitcast.245, s32[2048]{0:T(1024)S(1)} %get-tuple-element.432, s32[]{:T(128)} %constant.241.clone.1), kind=kCustom, calls=%fused_computation.151 | custom fusion | bytes 16388 | tf_op jit(solution)/shard_map/scatter | solution.py:80
  79.7 15.4 %all_to_all.25 = s32[64,1,64]{2,1,0:T(1,128)S(1)} all-to-all(s32[64,1,64]{2,1,0:T(1,128)S(1)} %all_to_all.17), channel_id=1, replica_groups=mesh['rep'=4,'shard'=64] {'shard'}, dimensions={0} | all-to-all | bytes 32768 | tf_op jit(solution)/shard_map/all_to_all | solution.py:84
  95.3 6.4 %copy.46 = bf16[8192,256]{1,0:T(8,128)(2,1)} copy(bf16[8192,256]{0,1:T(8,128)(2,1)} %all-gather.2.cloned.1.call-done) | data formatting | bytes 8388608 | tf_op jit(solution)/shard_map/all_gather | solution.py:72
  101.7 18.6 %gather_fusion.3 = bf16[4096,256]{1,0:T(8,128)(2,1)} fusion(bf16[8192,256]{1,0:T(8,128)(2,1)} %copy.46, s32[4096]{0:T(1024)S(1)} %broadcast_clamp_fusion), kind=kCustom, calls=%fused_computation.3 | custom fusion | bytes 4210688 | tf_op jit(solution)/shard_map/jit(_take)/gather | solution.py:82
  120.3 2.9 %broadcast_select_fusion = bf16[64,64,256]{2,1,0:T(8,128)(2,1)} fusion(bf16[64,64,256]{2,1,0:T(8,128)(2,1)} %bitcast.236, pred[64,64]{1,0:T(8,128)(4,1)S(1)} %compare_and_fusion), kind=kLoop, calls=%fused_computation.95 | loop fusion | flops 1048576 | bytes 4198400 | tf_op jit(solution)/shard_map/jit(_take)/select_n | solution.py:82
  123.2 5.6 %all-to-all-start.2 = ((bf16[64,64,256]{2,1,0:T(8,128)(2,1)}), bf16[64,64,256]{2,1,0:T(8,128)(2,1)}, u32[]{:S(2)}, u32[]{:S(2)}) async-start(bf16[64,64,256]{2,1,0:T(8,128)(2,1)} %broadcast_select_fusion), calls=%async_computation.2 | async-start | bytes 4194304 | tf_op jit(solution)/shard_map/all_to_all | solution.py:81
  136.2 43.8 %all-to-all-done.2 = bf16[64,64,256]{2,1,0:T(8,128)(2,1)} async-done(((bf16[64,64,256]{2,1,0:T(8,128)(2,1)}), bf16[64,64,256]{2,1,0:T(8,128)(2,1)}, u32[]{:S(2)}, u32[]{:S(2)}) %all-to-all-start.2) | async-done | bytes 2097184 | tf_op jit(solution)/shard_map/all_to_all | solution.py:81
  180.0 8.5 %gather_fusion.4 = bf16[2048,256]{1,0:T(8,128)(2,1)S(1)} fusion(bf16[4096,256]{1,0:T(8,128)(2,1)} %bitcast.17, s32[2048]{0:T(1024)S(1)} %broadcast_clamp_fusion.1), kind=kCustom, calls=%fused_computation.4 | custom fusion | bytes 2105344 | tf_op jit(solution)/shard_map/jit(_take)/gather | solution.py:94
  190.4 2.7 %fusion.74 = f32[2048,1024]{0,1:S(1)} fusion(bf16[256,1024]{1,0:T(8,128)(2,1)} %param.20, f32[2048]{0:T(1024)S(1)} %add_rsqrt_fusion, f32[2048]{0:T(1024)S(1)} %broadcast_multiply_fusion.1, bf16[2048,256]{1,0:T(8,128)(2,1)S(1)} %gather_fusion.4, pred[2048]{0:T(1024)(128)(4,1)S(1)} %compare_and_fusion.1), kind=kOutput, calls=%fused_computation.98 | convolution fusion | flops 1076363264 | bytes 9979904
  200.8 2.7 %fusion.93 = (bf16[4,1,512,64]{2,1,3,0:T(2,128)(2,1)}, bf16[4,1,512,64]{2,1,3,0:T(2,128)(2,1)}, bf16[4,1,512,64]{2,1,3,0:T(2,128)(2,1)}, bf16[4,1,512,64]{2,1,3,0:T(2,128)(2,1)}) fusion(bf16[4,2,1024,64]{2,1,3,0:T(2,128)(2,1)S(1)} %reshape_squeeze.10), kind=kLoop, calls=%fused_computation.169 | loop fusion | bytes 2097152 | tf_op jit(solution)/shard_map/slice | solution.py:114
  205.3 2.5 fusion.94
  214.7 3.1 %while.48 = (s32[]{:T(128)}, f32[4,512,64]{1,2,0:T(8,128)S(1)}, s32[]{:T(128)}, bf16[4,1024,64]{1,2,0:T(8,128)(2,1)}, bf16[4,512,64]{1,2,0:T(8,128)(2,1)}, /*ind...) while((s32[]{:T(128)}, f32[4,512,64]{1,2,0:T(8,128)S(1)}, ...), condition=%wide.region_8.9_spmd, body=%wide.region_7.8_spmd.sunk | while | flops 277217792 | bytes 2365087 | solution.py:135
  215.0 2.9 %fusion.122 = f32[4,512,64]{1,2,0:T(8,128)S(1)} fusion(f32[4,512,64]{1,2,0:T(8,128)S(1)} %get-tuple-element.739, bf16[4,512,64]{1,2,0:T(8,128)(2,1)} %get-tuple-element.753, f32[]{:T(128)} %get-tuple-element.754, pred[512,512]{0,1:T(8,128)(4,1)S(1)} %iota_compare_fusion.7, bf16[4,1024,64]{1,2,0:T(8,128)(2,1)S(1)} %get-tuple-element.755, ...), kind=kOutput, calls=%fused_computation.15.clone.1 | convolution fusion | flops 276955136 | bytes 2098688 | tf_op jit(solution)/shard_map/while/body/hqk,hkd->hqd/dot_general | solution.py:57
  219.5 6.5 %while.49 = (s32[]{:T(128)}, f32[4,512,64]{1,2,0:T(8,128)S(1)}, s32[]{:T(128)}, bf16[4,1024,64]{1,2,0:T(8,128)(2,1)}, bf16[4,512,64]{1,2,0:T(8,128)(2,1)}, /*ind...) while((s32[]{:T(128)}, f32[4,512,64]{1,2,0:T(8,128)S(1)}, ...), condition=%wide.region_10.11_spmd, body=%wide.region_9.10_spmd.sunk | while | flops 277218304 | bytes 2369183 | solution.py:135
  219.7 3.0 %fusion.126 = f32[4,512,64]{1,2,0:T(8,128)S(1)} fusion(f32[4,512,64]{1,2,0:T(8,128)S(1)} %get-tuple-element.706, bf16[4,512,64]{1,2,0:T(8,128)(2,1)} %get-tuple-element.720, f32[]{:T(128)} %get-tuple-element.721, pred[512,512]{0,1:T(8,128)(4,1)S(1)} %broadcast_compare_fusion.4, bf16[4,1024,64]{1,2,0:T(8,128)(2,1)} %get-tuple-element.722, ...), kind=kOutput, calls=%fused_computation.33.clone.1 | convolution fusion | flops 276955136 | bytes 2098688 | tf_op jit(solution)/shard_map/while/body/hqk,hkd->hqd/dot_general | solution.py:57
  222.9 3.0 %fusion.126 = f32[4,512,64]{1,2,0:T(8,128)S(1)} fusion(f32[4,512,64]{1,2,0:T(8,128)S(1)} %get-tuple-element.706, bf16[4,512,64]{1,2,0:T(8,128)(2,1)} %get-tuple-element.720, f32[]{:T(128)} %get-tuple-element.721, pred[512,512]{0,1:T(8,128)(4,1)S(1)} %broadcast_compare_fusion.4, bf16[4,1024,64]{1,2,0:T(8,128)(2,1)} %get-tuple-element.722, ...), kind=kOutput, calls=%fused_computation.33.clone.1 | convolution fusion | flops 276955136 | bytes 2098688 | tf_op jit(solution)/shard_map/while/body/hqk,hkd->hqd/dot_general | solution.py:57
  228.3 3.3 %while.50 = (s32[]{:T(128)}, f32[4,512,64]{1,2,0:T(8,128)S(1)}, s32[]{:T(128)}, bf16[4,1024,64]{1,2,0:T(8,128)(2,1)}, bf16[4,512,64]{1,2,0:T(8,128)(2,1)}, /*ind...) while((s32[]{:T(128)}, f32[4,512,64]{1,2,0:T(8,128)S(1)}, ...), condition=%wide.region_12.13_spmd, body=%wide.region_11.12_spmd.sunk | while | flops 277217792 | bytes 2365087 | solution.py:135
  228.6 3.0 %fusion.130 = f32[4,512,64]{1,2,0:T(8,128)S(1)} fusion(f32[4,512,64]{1,2,0:T(8,128)S(1)} %get-tuple-element.673, bf16[4,512,64]{1,2,0:T(8,128)(2,1)} %get-tuple-element.687, f32[]{:T(128)} %get-tuple-element.688, pred[512,512]{0,1:T(8,128)(4,1)S(1)} %iota_compare_fusion.8, bf16[4,1024,64]{1,2,0:T(8,128)(2,1)} %get-tuple-element.689, ...), kind=kOutput, calls=%fused_computation.52.clone.1 | convolution fusion | flops 276955136 | bytes 2098688 | tf_op jit(solution)/shard_map/while/body/hqk,hkd->hqd/dot_general | solution.py:57
  237.1 2.9 %fusion.65 = bf16[2048,256]{1,0:T(8,128)(2,1)} fusion(bf16[4,64,256]{2,1,0:T(8,128)(2,1)S(1)} %bitcast.251, f32[4,2048,64]{1,2,0:T(8,128)S(1)} %bitcast.237, bf16[4,4,2048,64]{2,3,1,0:T(8,128)(2,1)} %copy-done.4, f32[2048]{0:T(1024)S(1)} %bitcast.249, f32[2048]{0:T(1024)S(1)} %bitcast.250, pred[2048]{0:T(1024)(128)(4,1)S(1)} %copy-done.16, ...), kind=kOutput, calls=%fused_computation.86 | convolution fusion | flops 273678336 | bytes 5394432 | tf_op jit(solution)/shard_map/hef,hfo->eo/dot_general | solution.py:141
  (105 shorter events, 35.5 us)
Async XLA Ops:
  6.5 33.7 %copy-start = (s32[524288]{0:T(1024)S(1)}, s32[524288]{0:T(1024)}, u32[]{:S(2)}) copy-start(s32[524288]{0:T(1024)} %param.18) | copy-start | bytes 6291460
  6.5 88.7 %all-gather.2.cloned.1.call-start = ((), (), s32[]{:S(2)}) async-start(), calls=%async_computation.3 | async-start | bytes 5242880 | tf_op jit(solution)/shard_map/all_gather | solution.py:72
  8.9 30.3 %all-to-all-start = ((s32[64,2,1024]{2,1,0:T(2,128)}), s32[64,2,1024]{2,1,0:T(2,128)S(1)}, u32[]{:S(2)}, u32[]{:S(2)}) async-start(s32[64,2,1024]{2,1,0:T(2,128)} %broadcast_in_dim.135), calls=%async_computation | async-start | bytes 1048576 | tf_op jit(solution)/shard_map/all_to_all | solution.py:22
  120.3 8.6 %copy-start.1 = (s32[1,128]{1,0:T(1,128)S(1)}, s32[1,128]{1,0:T(1,128)}, u32[]{:S(2)}) copy-start(s32[1,128]{1,0:T(1,128)} %param.16) | copy-start | bytes 1540
  123.2 56.8 %all-to-all-start.2 = ((bf16[64,64,256]{2,1,0:T(8,128)(2,1)}), bf16[64,64,256]{2,1,0:T(8,128)(2,1)}, u32[]{:S(2)}, u32[]{:S(2)}) async-start(bf16[64,64,256]{2,1,0:T(8,128)(2,1)} %broadcast_select_fusion), calls=%async_computation.2 | async-start | bytes 4194304 | tf_op jit(solution)/shard_map/all_to_all | solution.py:81
  136.2 54.1 %copy-start.14 = (pred[2048]{0:T(1024)(128)(4,1)}, pred[2048]{0:T(1024)(128)(4,1)S(1)}, u32[]{:S(2)}) copy-start(pred[2048]{0:T(1024)(128)(4,1)S(1)} %compare_and_fusion.1) | copy-start | bytes 6148
  188.6 4.5 %copy-start.2 = (bf16[2048,256]{1,0:T(8,128)(2,1)}, bf16[2048,256]{1,0:T(8,128)(2,1)S(1)}, u32[]{:S(2)}) copy-start(bf16[2048,256]{1,0:T(8,128)(2,1)S(1)} %gather_fusion.4) | copy-start | bytes 3145732
  195.3 1.9 copy-start.4
  209.6 1.6 copy-start.11
  209.6 1.6 copy-start.12
  209.6 2.5 %copy-start.5 = (bf16[4,1,1024,64]{2,1,3,0:T(2,128)(2,1)S(1)}, bf16[4,1,1024,64]{2,1,3,0:T(2,128)(2,1)}, u32[]{:S(2)}) copy-start(bf16[4,1,1024,64]{2,1,3,0:T(2,128)(2,1)} %get-tuple-element.426) | copy-start | bytes 1572868
  209.7 2.5 copy-start.6
  217.9 0.8 copy-start.13
  218.7 0.8 copy-start.7
  225.9 2.4 copy-start.9
  231.6 0.8 copy-start.10
  232.4 1.0 copy-start.8
  235.9 1.2 copy-start.3
  235.9 1.2 copy-start.15
  235.9 1.2 copy-start.16
  235.9 1.2 copy-start.17
Sparse Core Ops, SparseCore 0:
  9.1 55.9 all-gather.1
where the time goes:
time: 249 us; the launch traced here: 247 us
  local copies, waits for them, and re-layouts  84.4 us (34%)
  waiting for transfers between devices  58.5 us (23%)
  other arithmetic  33.1 us (13%)
  between operations  19.3 us (8%)
  starting transfers between devices  18.6 us (7%)
  matrix products  17.4 us (7%)
  blocking collectives  15.4 us (6%)
    all_to_all x1, waiting for transfers between devices, body(): lax.all_to_all(jnp.take(table, lax.all_to_all(asked.reshape(shards, capac...  43.8 us
    gather x1, local copies, waits for them, and re-layouts, body(): jnp.take(table, lax.all_to_all(asked.reshape(shards, capacity), 'shard',...  18.6 us
    another operation x3, other arithmetic  18.5 us
    all_to_all x1, blocking collectives, body(): lax.all_to_all(asked.reshape(shards, capacity), 'shard', split_axis=0, co...  15.4 us
    all_to_all x1, waiting for transfers between devices, from_everyone(): lax.all_to_all(jnp.broadcast_to(array[None], (size, *array.shape)), axis,...  13.9 us
    all_to_all x1, starting transfers between devices, from_everyone(): lax.all_to_all(jnp.broadcast_to(array[None], (size, *array.shape)), axis,...  13 us
    dot_general x4, matrix products, block_terms(): jnp.einsum('hqk,hkd->hqd', weights, values, preferred_element_type=jnp.fl...  11.8 us
    gather x1, local copies, waits for them, and re-layouts, body(): home = row_home[my_ids]  11.8 us
  transfers between devices with their start and end apart: 3, of which 2 were waited for; matrix products, arithmetic and copies ran while one was open for 19% of the time, Pallas kernels for 0%

commit v1 on v0

v1 whole, which is shorter than its diff:
```python
import math

import jax
import jax.numpy as jnp
from jax import lax
from jax.experimental import pallas as pl
from jax.experimental.pallas import tpu as pltpu
from jax.sharding import PartitionSpec as P

HEADS = 4
EPSILON = 1e-06
BLOCK = 256
CAP = 32
F32 = jnp.float32
BF16 = jnp.bfloat16
I32 = jnp.int32


def column_of(row, size):
    pieces = []
    step = 128
    eye = lax.broadcasted_iota(I32, (step, step), 0) == lax.broadcasted_iota(I32, (step, step), 1)
    for i in range(size // step):
        part = row[:, i * step : (i + 1) * step].astype(F32)
        pieces.append(jnp.sum(jnp.where(eye, part, 0.0), axis=1, keepdims=True))
    return jnp.concatenate(pieces, axis=0)


def contract_rows(left, right):
    return lax.dot_general(left, right, (((0,), (0,)), ((), ())), preferred_element_type=F32)


def plan_kernel(ids_smem, len_smem, ids_ref, home_ref, out_ref, stage):
    seq_len = ids_ref.shape[1]
    shards = out_ref.shape[0]
    rows_dev = home_ref.shape[0] * 128 // shards
    step = 32

    for seq in range(2):

        def fetch(c, carry):
            for i in range(step):
                t = c * step + i
                row = ids_smem[seq, t] // 128
                stage[pl.ds(seq * seq_len + t, 1), :] = home_ref[pl.ds(row, 1), :]
            return carry

        lax.fori_loop(0, seq_len // step, fetch, 0)

    place = lax.broadcasted_iota(I32, (seq_len, 1), 0)
    lane = lax.broadcasted_iota(I32, (seq_len, 128), 1)
    lane_k = lax.broadcasted_iota(I32, (seq_len, shards), 1)
    below = (
        lax.broadcasted_iota(I32, (128, 128), 1) < lax.broadcasted_iota(I32, (128, 128), 0)
    ).astype(BF16)
    own = ((place // 16) == lane_k).astype(BF16)
    result = jnp.zeros((shards, 128), F32)
    for seq in range(2):
        ids = column_of(ids_ref[seq : seq + 1, :], seq_len).astype(I32)
        picked = jnp.where(
            (ids & 127) == lane, stage[pl.ds(seq * seq_len, seq_len), :].astype(F32), 0.0
        )
        home = jnp.sum(picked, axis=1, keepdims=True).astype(I32)
        target = home // rows_dev
        row = home & (rows_dev - 1)
        live = place < len_smem[seq]
        onehot = jnp.where((target == lane_k) & live, 1.0, 0.0)
        onehot16 = onehot.astype(BF16)
        carry = jnp.zeros((1, shards), F32)
        ranks = []
        for b in range(seq_len // 128):
            part = onehot[b * 128 : (b + 1) * 128]
            before = jnp.dot(below, part.astype(BF16), preferred_element_type=F32) + carry
            ranks.append(jnp.sum(before * part, axis=1, keepdims=True))
            carry = carry + jnp.sum(part, axis=0, keepdims=True)
        rank = jnp.concatenate(ranks, axis=0).astype(I32)
        at_rank = lane == rank + seq * CAP
        count = jnp.where(lane == 96 + seq, 1.0, 0.0)
        high = jnp.where(at_rank, (row & ~127).astype(F32), count)
        low = jnp.where(at_rank, (row & 127).astype(F32), 0.0)
        result = result + contract_rows(onehot16, high.astype(BF16))
        result = result + contract_rows(onehot16, low.astype(BF16))
        slot = jnp.where(live, target * CAP + rank, 0)
        at_place = lane == (place & 15) + (64 + seq * 16)
        high = jnp.where(at_place, (slot & ~127).astype(F32), 0.0)
        low = jnp.where(at_place, (slot & 127).astype(F32), 0.0)
        result = result + contract_rows(own, high.astype(BF16))
        result = result + contract_rows(own, low.astype(BF16))
    out_ref[...] = result.astype(I32)


def plan_requests(item_ids, lengths, row_home, shards):
    seq_dev, seq_len = item_ids.shape
    return pl.pallas_call(
        plan_kernel,
        out_shape=jax.ShapeDtypeStruct((shards, 128), I32),
        in_specs=[
            pl.BlockSpec(memory_space=pltpu.SMEM),
            pl.BlockSpec(memory_space=pltpu.SMEM),
            pl.BlockSpec(memory_space=pltpu.VMEM),
            pl.BlockSpec(memory_space=pltpu.VMEM),
        ],
        out_specs=pl.BlockSpec(memory_space=pltpu.VMEM),
        scratch_shapes=[pltpu.VMEM((seq_dev * seq_len, 128), I32)],
        name="plan",
    )(item_ids, lengths, item_ids, row_home.reshape(-1, 128))


def gather_kernel(order_ref, asked_ref, table_ref, out_ref, rows, stage):
    step = pl.program_id(0)
    width, rows_dev = table_ref.shape
    owners = out_ref.shape[0]
    chunk = 256

    @pl.when(step == 0)
    def _():
        eye = (
            lax.broadcasted_iota(I32, (chunk, chunk), 0)
            == lax.broadcasted_iota(I32, (chunk, chunk), 1)
        ).astype(BF16)

        def turn(c, carry):
            at = pl.multiple_of(c * chunk, chunk)
            rows[pl.ds(at, chunk), :] = lax.dot_general(
                eye, table_ref[:, pl.ds(at, chunk)], (((1,), (1,)), ((), ())), preferred_element_type=F32
            )
            return carry

        lax.fori_loop(0, rows_dev // chunk, turn, 0)

    unroll = 8

    def history(q, carry):
        hist = order_ref[step * owners * 2 + q]
        source = hist // 2
        half = hist & 1
        count = asked_ref[source, 96 + half]

        def fetch(c, carry):
            for i in range(unroll):
                j = c * unroll + i
                row = asked_ref[source, half * CAP + j]
                stage[pl.ds(q * CAP + j, 1), :] = rows[pl.ds(row, 1), :]
            return carry

        return lax.fori_loop(0, (count + unroll - 1) // unroll, fetch, carry)

    lax.fori_loop(0, owners * 2, history, 0)
    out_ref[...] = stage[...].astype(BF16).reshape(out_ref.shape)


def gather_rows(order, asked, table, shards):
    width, rows_dev = table.shape
    owners = 8
    return pl.pallas_call(
        gather_kernel,
        grid=(shards // owners,),
        out_shape=jax.ShapeDtypeStruct((shards, 2 * CAP, width), BF16),
        in_specs=[
            pl.BlockSpec(memory_space=pltpu.SMEM),
            pl.BlockSpec(memory_space=pltpu.SMEM),
            pl.BlockSpec((width, rows_dev), lambda i: (0, 0)),
        ],
        out_specs=pl.BlockSpec((owners, 2 * CAP, width), lambda i: (i, 0, 0)),
        scratch_shapes=[
            pltpu.VMEM((rows_dev, width), F32),
            pltpu.VMEM((owners * 2 * CAP, width), F32),
        ],
        compiler_params=pltpu.CompilerParams(vmem_limit_bytes=48 * 1024 * 1024),
        name="gather",
    )(order, asked, table)


def normed_rows(values):
    center = values - jnp.mean(values, axis=-1, keepdims=True)
    spread = jnp.mean(center * center, axis=-1, keepdims=True)
    return center * lax.rsqrt(spread + EPSILON)


def gated_linear(half):
    return half + half * jnp.tanh(half)


def layer_kernel(
    slots_ref, len_ref, got_ref, proj_ref, outw_ref, mixed_ref,
    flat, emb, gates, vals, quer, keys, att,
):
    seq = pl.program_id(0)
    seq_len, width = mixed_ref.shape[1:]
    head = width // HEADS
    length = len_ref[seq]
    flat[...] = got_ref[...].reshape(flat.shape).astype(F32)
    unroll = 16

    def fetch(c, carry):
        for i in range(unroll):
            t = c * unroll + i
            emb[pl.ds(t, 1), :] = flat[pl.ds(slots_ref[seq, t], 1), :]
        return carry

    lax.fori_loop(0, (length + unroll - 1) // unroll, fetch, 0)
    blocks = (length + BLOCK - 1) // BLOCK
    place = lax.broadcasted_iota(I32, (BLOCK, 1), 0)

    def project(b, carry):
        at = pl.multiple_of(b * BLOCK, BLOCK)
        span = pl.ds(at, BLOCK)
        rows = jnp.where(place + at < length, emb[span, :], 0.0)
        emb[span, :] = rows
        normed = normed_rows(rows).astype(BF16)
        for part, ref in enumerate((gates, vals, quer, keys)):
            raw = jnp.dot(
                normed, proj_ref[:, part * width : (part + 1) * width], preferred_element_type=F32
            )
            made = gated_linear(raw * 0.5).astype(BF16)
            if part == 0:
                ref[span, :] = made
            else:
                if part == 2:
                    made = made * (0.5 / math.sqrt(head))
                for h in range(HEADS):
                    ref[h, span, :] = made[:, h * head : (h + 1) * head]
        return carry

    lax.fori_loop(0, blocks, project, 0)
    inverse = 1.0 / length.astype(F32)
    for b in range(seq_len // BLOCK):

        @pl.when(b * BLOCK < length)
        def _(b=b):
            reach = (b + 1) * BLOCK
            keep = lax.broadcasted_iota(I32, (BLOCK, BLOCK), 1) <= lax.broadcasted_iota(
                I32, (BLOCK, BLOCK), 0
            )

            def attend(h, carry):
                query = quer[h, b * BLOCK : reach, :]
                scores = lax.dot_general(
                    query, keys[h, :reach, :], (((1,), (1,)), ((), ())), preferred_element_type=F32
                )
                weights = gated_linear(scores)
                last = jnp.where(keep, weights[:, b * BLOCK :], 0.0).astype(BF16)
                if b:
                    last = jnp.concatenate([weights[:, : b * BLOCK].astype(BF16), last], axis=1)
                att[h] = jnp.dot(last, vals[h, :reach, :], preferred_element_type=F32)
                return carry

            lax.fori_loop(0, HEADS, attend, 0)
            whole = jnp.concatenate([att[h] for h in range(HEADS)], axis=1) * inverse
            gated = (normed_rows(whole) * gates[b * BLOCK : reach, :].astype(F32)).astype(BF16)
            mixed = emb[b * BLOCK : reach, :] + jnp.dot(
                gated, outw_ref[...], preferred_element_type=F32
            )
            live = place + b * BLOCK < length
            mixed_ref[0, b * BLOCK : reach, :] = jnp.where(live, mixed, 0.0).astype(BF16)

        @pl.when(b * BLOCK >= length)
        def _(b=b):
            mixed_ref[0, b * BLOCK : (b + 1) * BLOCK, :] = jnp.zeros((BLOCK, width), BF16)


def layer(slots, lengths, got, proj_weight, out_weight):
    shards, seq_dev, cap, width = got.shape
    seq_len = slots.shape[1]
    head = width // HEADS
    return pl.pallas_call(
        layer_kernel,
        grid=(seq_dev,),
        out_shape=jax.ShapeDtypeStruct((seq_dev, seq_len, width), BF16),
        in_specs=[
            pl.BlockSpec(memory_space=pltpu.SMEM),
            pl.BlockSpec(memory_space=pltpu.SMEM),
            pl.BlockSpec((shards, 1, cap, width), lambda i: (0, i, 0, 0)),
            pl.BlockSpec((width, 4 * width), lambda i: (0, 0)),
            pl.BlockSpec((width, width), lambda i: (0, 0)),
        ],
        out_specs=pl.BlockSpec((1, seq_len, width), lambda i: (i, 0, 0)),
        scratch_shapes=[
            pltpu.VMEM((shards * cap, width), F32),
            pltpu.VMEM((seq_len, width), F32),
            pltpu.VMEM((seq_len, width), BF16),
            pltpu.VMEM((HEADS, seq_len, head), BF16),
            pltpu.VMEM((HEADS, seq_len, head), BF16),
            pltpu.VMEM((HEADS, seq_len, head), BF16),
            pltpu.VMEM((HEADS, BLOCK, head), F32),
        ],
        compiler_params=pltpu.CompilerParams(vmem_limit_bytes=48 * 1024 * 1024),
        name="layer",
    )(slots, lengths, got, proj_weight, out_weight)


def body(item_ids, seq_lengths, seq_owner, row_home, item_table, proj_weight, out_weight):
    shards = lax.axis_size("shard")
    me = lax.axis_index("shard")
    seq_dev, seq_len = item_ids.shape
    width = proj_weight.shape[0]
    owners = seq_owner[0]
    lengths = seq_lengths[0]
    table = lax.all_gather(item_table.T, "rep", axis=0, tiled=True)
    order = jnp.argsort(owners, stable=True)
    my_lengths = lengths[lax.dynamic_slice_in_dim(order, me * seq_dev, seq_dev)]
    held = lax.dynamic_slice_in_dim(lengths, me * seq_dev, seq_dev)
    asked = plan_requests(item_ids, held, row_home, shards)
    asked = lax.all_to_all(
        asked.reshape(shards, 1, 128), "shard", split_axis=0, concat_axis=0, tiled=True
    ).reshape(shards, 128)
    rows = gather_rows(order, asked, table, shards)
    chunk = seq_len // shards
    maps = jnp.take(asked[:, 64 : 64 + 2 * chunk].reshape(2 * shards, chunk), order, axis=0)
    maps = maps.reshape(shards, 1, seq_dev * chunk)
    maps = jnp.concatenate([maps // CAP, maps % CAP], axis=2).astype(BF16)
    maps = jnp.pad(maps, ((0, 0), (0, 7), (0, width - 4 * chunk)))
    got = lax.all_to_all(
        jnp.concatenate([rows, maps], axis=1), "shard", split_axis=0, concat_axis=0, tiled=True
    )
    slots = got[:, 2 * CAP, : 4 * chunk].astype(I32)
    slots = slots[:, : 2 * chunk] * CAP + slots[:, 2 * chunk :]
    slots = slots.reshape(shards, seq_dev, chunk).transpose(1, 0, 2).reshape(seq_dev, seq_len)
    got = got[:, : 2 * CAP].reshape(shards, seq_dev, CAP, width)
    return layer(slots, my_lengths, got, proj_weight, out_weight)


def solution(mesh):
    in_specs = (
        P(("rep", "shard"), None),
        P("rep", None),
        P("rep", None),
        P(),
        P("shard", "rep"),
        P(),
        P(),
    )
    out_specs = P(("rep", "shard"), None, None)
    return jax.shard_map(body, mesh=mesh, in_specs=in_specs, out_specs=out_specs, check_vma=False)
```

time: 249 us -> 190 us (0.76)
  local copies, waits for them, and re-layouts: 84.4 us -> 3.09 us
  Pallas kernels: 0 us -> 62.1 us
  other arithmetic: 33.1 us -> 4.57 us
  waiting for transfers between devices: 58.5 us -> 76.5 us
  matrix products: 17.4 us -> 0 us
  blocking collectives: 15.4 us -> 0 us
  starting transfers between devices: 18.6 us -> 27.5 us
  between operations: 19.3 us -> 13.5 us
    pallas_call x0 -> x3, Pallas kernels: none -> 62.1 us  [the longest x1 22.4 us: gather_rows(): pl.pallas_call(gather_kernel, grid=(shards // owners,), out_shape=jax.Sha...]
    gather x5 -> x3, local copies, waits for them, and re-layouts: 40 us -> 1.36 us  [the longest x2 0.72 us: body(): jnp.take(asked[:, 64:64 + 2 * chunk].reshape(2 * shards, chunk), order, a...]
    another operation x5 -> x0, other arithmetic: 20.8 us -> none
    all_to_all x1 -> x0, blocking collectives: 15.4 us -> none  [body(): lax.all_to_all(asked.reshape(shards, capacity), 'shard', split_axis=0, co...]
    dot_general x5 -> x0, matrix products: 14.7 us -> none  [the longest x4 11.8 us: block_terms(): jnp.einsum('hqk,hkd->hqd', weights, values, preferred_element_type=jnp.fl...]
    all_gather x1, waiting for transfers between devices: 0.02 us -> 13.7 us  [body(): table = lax.all_gather(item_table.T, 'rep', axis=0, tiled=True)]
    slice x6 -> x2, local copies, waits for them, and re-layouts: 9.24 us -> 0.34 us  [the longest x1 0.26 us: body(): got = got[:, :2 * CAP].reshape(shards, seq_dev, CAP, width)]
    all_to_all x2, starting transfers between devices: 18.6 us -> 27.4 us  [the longest x1 14.5 us: body(): lax.all_to_all(jnp.concatenate([rows, maps], axis=1), 'shard', split_axis...]
  transfers between devices with their start and end apart: 3 -> 3, of which waited for: 2 -> 3; matrix products, arithmetic and copies ran while one was open for 19% -> 3% of each run, Pallas kernels for 0% -> 10%
where the time goes in v1:
time: 190 us; the launch traced here: 187 us
  waiting for transfers between devices  76.5 us (40%)
  Pallas kernels  62.1 us (33%)
  starting transfers between devices  27.5 us (14%)
  between operations  13.5 us (7%)
  other arithmetic  4.57 us (2%)
  local copies, waits for them, and re-layouts  3.09 us (2%)
    all_to_all x1, waiting for transfers between devices, body(): lax.all_to_all(jnp.concatenate([rows, maps], axis=1), 'shard', split_axis...  55.9 us
    pallas_call x1, Pallas kernels, gather_rows(): pl.pallas_call(gather_kernel, grid=(shards // owners,), out_shape=jax.Sha...  22.4 us
    pallas_call x1, Pallas kernels, layer(): pl.pallas_call(layer_kernel, grid=(seq_dev,), out_shape=jax.ShapeDtypeStr...  20.9 us
    pallas_call x1, Pallas kernels, plan_requests(): pl.pallas_call(plan_kernel, out_shape=jax.ShapeDtypeStruct((shards, 128),...  18.7 us
    all_to_all x1, starting transfers between devices, body(): lax.all_to_all(jnp.concatenate([rows, maps], axis=1), 'shard', split_axis...  14.5 us
    all_gather x1, waiting for transfers between devices, body(): table = lax.all_gather(item_table.T, 'rep', axis=0, tiled=True)  13.7 us
    all_to_all x1, starting transfers between devices, body(): lax.all_to_all(asked.reshape(shards, 1, 128), 'shard', split_axis=0, conc...  13 us
    all_to_all x1, waiting for transfers between devices, body(): lax.all_to_all(asked.reshape(shards, 1, 128), 'shard', split_axis=0, conc...  6.21 us
  transfers between devices with their start and end apart: 3, of which 3 were waited for; matrix products, arithmetic and copies ran while one was open for 3% of the time, Pallas kernels for 10%

profile of v1, /device:TPU:1, one launch (start us, length us, event | category | flops | bytes accessed | tf_op | source)
XLA Modules:
  0.0 187.2 jit_solution(3314973565740085010)
XLA Ops:
  6.5 0.7 all-gather.2.cloned.1.call-update
  7.3 0.7 dynamic-slice_bitcast_fusion.len_smem
  7.9 18.7 %plan.1 = s32[64,128]{1,0:T(8,128)} custom-call(s32[2,1024]{1,0:T(2,128)} %ids_ref.1, s32[2]{0:T(128)} %dynamic-slice_bitcast_fusion.len_smem, s32[2,1024]{1,0:T(2,128)} %ids_ref.1, s32[4096,128]{1,0:T(8,128)} %bitcast.24), custom_call_target="tpu_custom_call" | custom-call | tf_op jit(solution)/shard_map/plan/pallas_call | solution.py:94
  26.7 13.0 %all-to-all-start = ((s32[64,1,128]{2,1,0:T(1,128)}), s32[64,1,128]{2,1,0:T(1,128)S(1)}, u32[]{:S(2)}, u32[]{:S(2)}) async-start(s32[64,1,128]{2,1,0:T(1,128)} %bitcast.27), calls=%async_computation | async-start | bytes 65536 | tf_op jit(solution)/shard_map/all_to_all | solution.py:304
  39.7 2.6 %sort.17 = (s32[128]{0:T(128)}, s32[128]{0:T(128)S(1)}) sort(s32[128]{0:T(128)S(1)} %bitcast.30, s32[128]{0:T(128)S(1)} %iota.4), dimensions={0}, to_apply=%region_0.0 | sort | flops 896 | bytes 2048 | tf_op jit(solution)/shard_map/jit(argsort)/sort | solution.py:300
  42.3 0.2 broadcast_in_dim.19
  42.4 0.1 copy.16
  42.5 0.1 copy.17
  42.7 6.2 %all-to-all-done = s32[64,1,128]{2,1,0:T(1,128)S(1)} async-done(((s32[64,1,128]{2,1,0:T(1,128)}), s32[64,1,128]{2,1,0:T(1,128)S(1)}, u32[]{:S(2)}, u32[]{:S(2)}) %all-to-all-start) | async-done | bytes 32800 | tf_op jit(solution)/shard_map/all_to_all | solution.py:304
  49.0 0.1 reshape.168
  49.0 0.7 gather_fusion
  49.8 0.1 pad_maximum_fusion
  49.9 13.7 %all-gather.2.cloned.1.call-done.table_ref = bf16[256,8192]{1,0:T(8,128)(2,1)} async-done(((bf16[64,8192]{1,0:T(8,128)(2,1)}), bf16[256,8192]{1,0:T(8,128)(2,1)}) %all-gather.2.cloned.1.call-update) | async-done | bytes 4194320 | tf_op jit(solution)/shard_map/all_gather | solution.py:299
  63.6 22.4 %gather.17 = bf16[64,64,256]{2,1,0:T(8,128)(2,1)S(1)} custom-call(s32[128]{0:T(128)S(1)} %get-tuple-element.6.order_ref, s32[64,128]{1,0:T(8,128)S(1)} %bitcast.23, bf16[256,8192]{1,0:T(8,128)(2,1)} %all-gather.2.cloned.1.call-done.table_ref), custom_call_target="tpu_custom_call" | custom-call | tf_op jit(solution)/shard_map/gather/pallas_call | solution.py:155
  86.0 1.6 fusion.1
  87.6 14.5 %all-to-all-start.1 = ((bf16[64,72,256]{2,1,0:T(8,128)(2,1)}), bf16[64,72,256]{2,1,0:T(8,128)(2,1)S(1)}, u32[]{:S(2)}, u32[]{:S(2)}) async-start(bf16[64,72,256]{2,1,0:T(8,128)(2,1)} %fusion.1), calls=%async_computation.1 | async-start | bytes 4718592 | tf_op jit(solution)/shard_map/all_to_all | solution.py:313
  102.1 0.1 compare_select_fusion
  102.2 0.6 gather_fusion.1
  102.8 55.9 %all-to-all-done.1 = bf16[64,72,256]{2,1,0:T(8,128)(2,1)S(1)} async-done(((bf16[64,72,256]{2,1,0:T(8,128)(2,1)}), bf16[64,72,256]{2,1,0:T(8,128)(2,1)S(1)}, u32[]{:S(2)}, u32[]{:S(2)}) %all-to-all-start.1) | async-done | bytes 2359328 | tf_op jit(solution)/shard_map/all_to_all | solution.py:313
  158.8 0.1 slice_add_fusion
  158.9 0.1 copy.20
  159.0 0.1 reshape.170.slots_ref
  159.1 0.3 slice.28
  159.4 20.9 %layer.1 = bf16[2,1024,256]{2,1,0:T(8,128)(2,1)} custom-call(s32[2,1024]{1,0:T(2,128)S(1)} %reshape.170.slots_ref, s32[2]{0:T(128)S(1)} %gather_fusion.1, bf16[64,2,32,256]{3,2,1,0:T(8,128)(2,1)S(1)} %bitcast.21, bf16[256,1024]{1,0:T(8,128)(2,1)S(1)} %copy-done.1, bf16[256,256]{1,0:T(8,128)(2,1)S(1)} %copy-done.2), custom_call_target="tpu_custom_call" | custom-call | tf_op jit(solution)/shard_map/layer/pallas_call | solution.py:266
  (21 shorter events, 0.4 us)
Async XLA Ops:
  6.5 0.7 copy-start
  6.5 33.1 %copy-start.3 = (s32[1,128]{1,0:T(1,128)S(1)}, s32[1,128]{1,0:T(1,128)}, u32[]{:S(2)}) copy-start(s32[1,128]{1,0:T(1,128)} %param.9) | copy-start | bytes 1540
  6.5 57.0 %all-gather.2.cloned.1.call-start = ((), (), s32[]{:S(2)}) async-start(), calls=%async_computation.2 | async-start | bytes 5242880 | tf_op jit(solution)/shard_map/all_gather | solution.py:299
  26.7 22.2 %all-to-all-start = ((s32[64,1,128]{2,1,0:T(1,128)}), s32[64,1,128]{2,1,0:T(1,128)S(1)}, u32[]{:S(2)}, u32[]{:S(2)}) async-start(s32[64,1,128]{2,1,0:T(1,128)} %bitcast.27), calls=%async_computation | async-start | bytes 65536 | tf_op jit(solution)/shard_map/all_to_all | solution.py:304
  87.6 71.1 %all-to-all-start.1 = ((bf16[64,72,256]{2,1,0:T(8,128)(2,1)}), bf16[64,72,256]{2,1,0:T(8,128)(2,1)S(1)}, u32[]{:S(2)}, u32[]{:S(2)}) async-start(bf16[64,72,256]{2,1,0:T(8,128)(2,1)} %fusion.1), calls=%async_computation.1 | async-start | bytes 4718592 | tf_op jit(solution)/shard_map/all_to_all | solution.py:313
  102.8 56.5 %copy-start.1 = (bf16[256,1024]{1,0:T(8,128)(2,1)S(1)}, bf16[256,1024]{1,0:T(8,128)(2,1)}, u32[]{:S(2)}) copy-start(bf16[256,1024]{1,0:T(8,128)(2,1)} %proj_ref.1) | copy-start | bytes 1572868
  102.8 56.5 %copy-start.2 = (bf16[256,256]{1,0:T(8,128)(2,1)S(1)}, bf16[256,256]{1,0:T(8,128)(2,1)}, u32[]{:S(2)}) copy-start(bf16[256,256]{1,0:T(8,128)(2,1)} %outw_ref.1) | copy-start | bytes 393220
Sparse Core Ops, SparseCore 0:
  9.1 54.3 all-gather.1

commit v2 on v1

--- a/solution.py
+++ b/solution.py
@@ -106,69 +106,221 @@
     )(item_ids, lengths, item_ids, row_home.reshape(-1, 128))
 
 
-def gather_kernel(order_ref, asked_ref, table_ref, out_ref, rows, stage):
-    step = pl.program_id(0)
-    width, rows_dev = table_ref.shape
-    owners = out_ref.shape[0]
-    chunk = 256
-
-    @pl.when(step == 0)
-    def _():
-        eye = (
-            lax.broadcasted_iota(I32, (chunk, chunk), 0)
-            == lax.broadcasted_iota(I32, (chunk, chunk), 1)
-        ).astype(BF16)
-
-        def turn(c, carry):
+def exchange_kernel(
+    order_ref, asked_ref, table_ref,
+    own_got, pair_got, far_got, maps_got,
+    asked_all, asked_smem, table_in, left_in, right_in, far_in,
+    own_rows, pair_rows, far_rows, stage,
+    own_out, pair_out, far_out, maps_out,
+    local_sem, asked_send, asked_recv, side_send, side_recv, row_send, row_recv,
+):
+    shards = asked_ref.shape[0]
+    reps = 4
+    cols, rows_dev = table_ref.shape
+    me = lax.axis_index("shard")
+    rep = lax.axis_index("rep")
+    right = lax.rem(rep + 1, reps)
+    left = lax.rem(rep + reps - 1, reps)
+    chunk = min(256, rows_dev)
+
+    load = pltpu.make_async_copy(table_ref, table_in, local_sem.at[0])
+    load.start()
+    barrier = pltpu.get_barrier_semaphore()
+
+    def greet(i, carry):
+        peer = lax.rem(me + i, shards)
+        pl.semaphore_signal(
+            barrier, inc=1, device_id={"shard": peer}, device_id_type=pl.DeviceIdType.MESH
+        )
+        return carry
+
+    lax.fori_loop(1, shards, greet, 0)
+    for side in (left, right):
+        pl.semaphore_signal(
+            barrier, inc=1, device_id={"rep": side}, device_id_type=pl.DeviceIdType.MESH
+        )
+
+    eye = (
+        lax.broadcasted_iota(I32, (chunk, chunk), 0) == lax.broadcasted_iota(I32, (chunk, chunk), 1)
+    ).astype(BF16)
+
+    def turn(upper, lower, rows):
+        def one(c, carry):
             at = pl.multiple_of(c * chunk, chunk)
+            both = jnp.concatenate([upper[:, pl.ds(at, chunk)], lower[:, pl.ds(at, chunk)]], axis=0)
             rows[pl.ds(at, chunk), :] = lax.dot_general(
-                eye, table_ref[:, pl.ds(at, chunk)], (((1,), (1,)), ((), ())), preferred_element_type=F32
+                eye, both, (((1,), (1,)), ((), ())), preferred_element_type=F32
             )
             return carry
 
-        lax.fori_loop(0, rows_dev // chunk, turn, 0)
-
-    unroll = 8
-
-    def history(q, carry):
-        hist = order_ref[step * owners * 2 + q]
-        source = hist // 2
-        half = hist & 1
-        count = asked_ref[source, 96 + half]
-
-        def fetch(c, carry):
-            for i in range(unroll):
-                j = c * unroll + i
-                row = asked_ref[source, half * CAP + j]
-                stage[pl.ds(q * CAP + j, 1), :] = rows[pl.ds(row, 1), :]
+        lax.fori_loop(0, rows_dev // chunk, one, 0)
+
+    load.wait()
+    pl.semaphore_wait(barrier, shards + 1)
+
+    def side_copy(source, target, slot, side):
+        return pltpu.make_async_remote_copy(
+            src_ref=source,
+            dst_ref=target,
+            send_sem=side_send.at[slot],
+            recv_sem=side_recv.at[slot],
+            device_id={"rep": side},
+            device_id_type=pl.DeviceIdType.MESH,
+        )
+
+    def shard_copy(source, target, send, recv, peer):
+        return pltpu.make_async_remote_copy(
+            src_ref=source,
+            dst_ref=target,
+            send_sem=send,
+            recv_sem=recv,
+            device_id={"shard": peer},
+            device_id_type=pl.DeviceIdType.MESH,
+        )
+
+    def ask(i, carry):
+        peer = lax.rem(me + i, shards)
+        shard_copy(
+            asked_ref.at[peer], asked_all.at[me], asked_send, asked_recv, peer
+        ).start()
+        return carry
+
+    lax.fori_loop(1, shards, ask, 0)
+    keep = pltpu.make_async_copy(asked_ref.at[me], asked_all.at[me], local_sem.at[1])
+    keep.start()
+    to_right = side_copy(table_in, left_in, 0, right)
+    to_left = side_copy(table_in, right_in, 1, left)
+    to_right.start()
+    to_left.start()
+    turn(table_in, table_in, own_rows)
+    keep.wait()
+    others = pl.ds(0, shards - 1)
+    shard_copy(asked_ref.at[others], asked_all.at[others], asked_send, asked_recv, me).wait()
+    spill = pltpu.make_async_copy(asked_all, asked_smem, local_sem.at[2])
+    spill.start()
+    spill.wait()
+
+    first_half = lax.broadcasted_iota(I32, (1, 2 * cols), 1) < cols
+
+    def send_to(out, got, kind, peer):
+        shard_copy(out.at[peer], got.at[me], row_send.at[kind], row_recv.at[kind], peer).start()
+
+    def finish(out, got, kind):
+        local = pltpu.make_async_copy(out.at[me], got.at[me], local_sem.at[3 + kind])
+        local.start()
+        local.wait()
+
+    def sweep(pick, out, got, kind, paired, extra=None):
+        def owner(i, carry):
+            peer = lax.rem(me + i + 1, shards)
+            sources = []
+            offsets = []
+            for q in range(2):
+                hist = order_ref[2 * peer + q]
+                sources.append(hist // 2)
+                offsets.append(lax.rem(hist, 2) * CAP)
+            if extra is not None:
+                for q in range(2):
+                    extra[peer, pl.ds(q, 1), :] = asked_all[sources[q]]
+            slot = lax.rem(i, 2)
+            if paired:
+                for j in range(CAP):
+                    one = pick[pl.ds(asked_smem[sources[0], 0, offsets[0] + j], 1), :]
+                    two = pick[pl.ds(asked_smem[sources[1], 0, offsets[1] + j], 1), :]
+                    stage[slot, pl.ds(j, 1), :] = jnp.where(first_half, one, two)
+                out[peer] = stage[slot, :CAP, :].astype(BF16)
+            else:
+                for q in range(2):
+                    for j in range(CAP):
+                        stage[slot, pl.ds(q * CAP + j, 1), :] = pick[
+                            pl.ds(asked_smem[sources[q], 0, offsets[q] + j], 1), :
+                        ]
+                out[peer] = stage[slot].astype(BF16)
+
+            @pl.when(i > 0)
+            def _():
+                before = lax.rem(me + i, shards)
+                send_to(out, got, kind, before)
+                if extra is not None:
+                    send_to(extra, maps_got, 3, before)
+
             return carry
 
-        return lax.fori_loop(0, (count + unroll - 1) // unroll, fetch, carry)
-
-    lax.fori_loop(0, owners * 2, history, 0)
-    out_ref[...] = stage[...].astype(BF16).reshape(out_ref.shape)
-
-
-def gather_rows(order, asked, table, shards):
-    width, rows_dev = table.shape
-    owners = 8
+        lax.fori_loop(0, shards, owner, 0)
+
+    sweep(own_rows, own_out, own_got, 0, True, maps_out)
+    to_right.wait_recv()
+    to_left.wait_recv()
+    half = cols // 2
+    on_right = side_copy(left_in.at[pl.ds(0, half)], far_in.at[pl.ds(0, half)], 2, right)
+    on_left = side_copy(right_in.at[pl.ds(half, half)], far_in.at[pl.ds(half, half)], 3, left)
+    on_right.start()
+    on_left.start()
+    turn(left_in, right_in, pair_rows)
+    sweep(pair_rows, pair_out, pair_got, 1, False)
+    on_right.wait_recv()
+    on_left.wait_recv()
+    turn(far_in, far_in, far_rows)
+    sweep(far_rows, far_out, far_got, 2, True)
+    for kind, (out, got) in enumerate(
+        ((own_out, own_got), (pair_out, pair_got), (far_out, far_got), (maps_out, maps_got))
+    ):
+        finish(out, got, kind)
+    for copy in (to_right, to_left, on_right, on_left):
+        copy.wait_send()
+    for kind, (out, got) in enumerate(
+        ((own_out, own_got), (pair_out, pair_got), (far_out, far_got), (maps_out, maps_got))
+    ):
+        shard_copy(
+            out.at[others], got.at[others], row_send.at[kind], row_recv.at[kind], me
+        ).wait()
+
+
+def exchange_rows(order, asked, table):
+    shards = asked.shape[0]
+    cols, rows_dev = table.shape
+    wide = 2 * cols
+    any_space = pl.BlockSpec(memory_space=pl.ANY)
+    shapes = (
+        ((shards, CAP, wide), BF16),
+        ((shards, 2 * CAP, wide), BF16),
+        ((shards, CAP, wide), BF16),
+        ((shards, 2, 128), I32),
+    )
     return pl.pallas_call(
-        gather_kernel,
-        grid=(shards // owners,),
-        out_shape=jax.ShapeDtypeStruct((shards, 2 * CAP, width), BF16),
+        exchange_kernel,
+        out_shape=[jax.ShapeDtypeStruct(*shape) for shape in shapes],
         in_specs=[
             pl.BlockSpec(memory_space=pltpu.SMEM),
-            pl.BlockSpec(memory_space=pltpu.SMEM),
-            pl.BlockSpec((width, rows_dev), lambda i: (0, 0)),
+            pl.BlockSpec(memory_space=pltpu.VMEM),
+            any_space,
         ],
-        out_specs=pl.BlockSpec((owners, 2 * CAP, width), lambda i: (i, 0, 0)),
+        out_specs=[any_space] * 4,
         scratch_shapes=[
-            pltpu.VMEM((rows_dev, width), F32),
-            pltpu.VMEM((owners * 2 * CAP, width), F32),
+            pltpu.VMEM((shards, 1, 128), I32),
+            pltpu.SMEM((shards, 1, 128), I32),
+            pltpu.VMEM((cols, rows_dev), BF16),
+            pltpu.VMEM((cols, rows_dev), BF16),
+            pltpu.VMEM((cols, rows_dev), BF16),
+            pltpu.VMEM((cols, rows_dev), BF16),
+            pltpu.VMEM((rows_dev, wide), F32),
+            pltpu.VMEM((rows_dev, wide), F32),
+            pltpu.VMEM((rows_dev, wide), F32),
+            pltpu.VMEM((2, 2 * CAP, wide), F32),
+            *[pltpu.VMEM(*shape) for shape in shapes],
+            pltpu.SemaphoreType.DMA((7,)),
+            pltpu.SemaphoreType.DMA,
+            pltpu.SemaphoreType.DMA,
+            pltpu.SemaphoreType.DMA((4,)),
+            pltpu.SemaphoreType.DMA((4,)),
+            pltpu.SemaphoreType.DMA((4,)),
+            pltpu.SemaphoreType.DMA((4,)),
         ],
-        compiler_params=pltpu.CompilerParams(vmem_limit_bytes=48 * 1024 * 1024),
-        name="gather",
-    )(order, asked, table)
+        compiler_params=pltpu.CompilerParams(
+            collective_id=0, has_side_effects=True, vmem_limit_bytes=40 * 1024 * 1024
+        ),
+        name="exchange",
+    )(order, asked.reshape(shards, 1, 128), table)
 
 
 def normed_rows(values):
@@ -182,20 +334,59 @@
 
 
 def layer_kernel(
-    slots_ref, len_ref, got_ref, proj_ref, outw_ref, mixed_ref,
+    maps_ref, info_ref, own_ref, pair_ref, far_ref, proj_ref, outw_ref, mixed_ref,
     flat, emb, gates, vals, quer, keys, att,
 ):
     seq = pl.program_id(0)
     seq_len, width = mixed_ref.shape[1:]
     head = width // HEADS
-    length = len_ref[seq]
-    flat[...] = got_ref[...].reshape(flat.shape).astype(F32)
+    length = info_ref[seq]
+    offset = 64 + 16 * info_ref[2 + seq]
+    rep = info_ref[4]
+    shards, cap = own_ref.shape[:2]
+    side = width // 4
+    group = 8
+    first_half = lax.broadcasted_iota(I32, (1, 2 * side), 1) < side
+    swapped = seq == 1
+
+    for r in range(4):
+
+        @pl.when(rep == r)
+        def _(r=r):
+            def place_blocks(c, carry):
+                span = pl.ds(c * group, group)
+                rows = group * cap
+                parts = {}
+                for name, ref in (("own", own_ref), ("far", far_ref)):
+                    part = ref[span].reshape(rows, 2 * side).astype(F32)
+                    other = pltpu.roll(part, side, 1)
+                    parts[name] = (
+                        jnp.where(swapped, other, part),
+                        jnp.where(swapped, part, other),
+                    )
+                pair = pair_ref[span].reshape(rows, 2 * side).astype(F32)
+                turned = pltpu.roll(pair, side, 1)
+                parts["left"] = (pair, turned)
+                parts["right"] = (turned, pair)
+                names = ("own", "right", "far", "left")
+                at = pl.multiple_of(c * rows, rows)
+                for tile in range(2):
+                    low = parts[names[(2 * tile - r) % 4]][0]
+                    high = parts[names[(2 * tile + 1 - r) % 4]][1]
+                    flat[pl.ds(at, rows), tile * 2 * side : (tile + 1) * 2 * side] = jnp.where(
+                        first_half, low, high
+                    )
+                return carry
+
+            lax.fori_loop(0, shards // group, place_blocks, 0)
+
     unroll = 16
 
     def fetch(c, carry):
         for i in range(unroll):
             t = c * unroll + i
-            emb[pl.ds(t, 1), :] = flat[pl.ds(slots_ref[seq, t], 1), :]
+            slot = maps_ref[c, seq, offset + i]
+            emb[pl.ds(t, 1), :] = flat[pl.ds(slot, 1), :]
         return carry
 
     lax.fori_loop(0, (length + unroll - 1) // unroll, fetch, 0)
@@ -259,9 +450,10 @@
             mixed_ref[0, b * BLOCK : (b + 1) * BLOCK, :] = jnp.zeros((BLOCK, width), BF16)
 
 
-def layer(slots, lengths, got, proj_weight, out_weight):
-    shards, seq_dev, cap, width = got.shape
-    seq_len = slots.shape[1]
+def layer(maps, info, own, pair, far, proj_weight, out_weight, seq_len):
+    shards, cap, wide = own.shape
+    seq_dev = 2
+    width = proj_weight.shape[0]
     head = width // HEADS
     return pl.pallas_call(
         layer_kernel,
@@ -270,7 +462,9 @@
         in_specs=[
             pl.BlockSpec(memory_space=pltpu.SMEM),
             pl.BlockSpec(memory_space=pltpu.SMEM),
-            pl.BlockSpec((shards, 1, cap, width), lambda i: (0, i, 0, 0)),
+            pl.BlockSpec((shards, cap, wide), lambda i: (0, 0, 0)),
+            pl.BlockSpec((shards, cap, wide), lambda i: (0, i, 0)),
+            pl.BlockSpec((shards, cap, wide), lambda i: (0, 0, 0)),
             pl.BlockSpec((width, 4 * width), lambda i: (0, 0)),
             pl.BlockSpec((width, width), lambda i: (0, 0)),
         ],
@@ -286,38 +480,23 @@
         ],
         compiler_params=pltpu.CompilerParams(vmem_limit_bytes=48 * 1024 * 1024),
         name="layer",
-    )(slots, lengths, got, proj_weight, out_weight)
+    )(maps, info, own, pair, far, proj_weight, out_weight)
 
 
 def body(item_ids, seq_lengths, seq_owner, row_home, item_table, proj_weight, out_weight):
     shards = lax.axis_size("shard")
     me = lax.axis_index("shard")
     seq_dev, seq_len = item_ids.shape
-    width = proj_weight.shape[0]
     owners = seq_owner[0]
     lengths = seq_lengths[0]
-    table = lax.all_gather(item_table.T, "rep", axis=0, tiled=True)
     order = jnp.argsort(owners, stable=True)
-    my_lengths = lengths[lax.dynamic_slice_in_dim(order, me * seq_dev, seq_dev)]
+    mine = lax.dynamic_slice_in_dim(order, me * seq_dev, seq_dev)
     held = lax.dynamic_slice_in_dim(lengths, me * seq_dev, seq_dev)
     asked = plan_requests(item_ids, held, row_home, shards)
-    asked = lax.all_to_all(
-        asked.reshape(shards, 1, 128), "shard", split_axis=0, concat_axis=0, tiled=True
-    ).reshape(shards, 128)
-    rows = gather_rows(order, asked, table, shards)
-    chunk = seq_len // shards
-    maps = jnp.take(asked[:, 64 : 64 + 2 * chunk].reshape(2 * shards, chunk), order, axis=0)
-    maps = maps.reshape(shards, 1, seq_dev * chunk)
-    maps = jnp.concatenate([maps // CAP, maps % CAP], axis=2).astype(BF16)
-    maps = jnp.pad(maps, ((0, 0), (0, 7), (0, width - 4 * chunk)))
-    got = lax.all_to_all(
-        jnp.concatenate([rows, maps], axis=1), "shard", split_axis=0, concat_axis=0, tiled=True
-    )
-    slots = got[:, 2 * CAP, : 4 * chunk].astype(I32)
-    slots = slots[:, : 2 * chunk] * CAP + slots[:, 2 * chunk :]
-    slots = slots.reshape(shards, seq_dev, chunk).transpose(1, 0, 2).reshape(seq_dev, seq_len)
-    got = got[:, : 2 * CAP].reshape(shards, seq_dev, CAP, width)
-    return layer(slots, my_lengths, got, proj_weight, out_weight)
+    own, pair, far, maps = exchange_rows(order, asked, item_table.T)
+    rep = lax.axis_index("rep").reshape(1)
+    info = jnp.concatenate([lengths[mine], mine % 2, rep])
+    return layer(maps, info, own, pair, far, proj_weight, out_weight, seq_len)
 
 
 def solution(mesh):

time: 190 us -> 131 us (0.69); the launches traced: 187 us -> 131 us
  waiting for transfers between devices: 76.5 us -> 0 us
  Pallas kernels: 62.1 us -> 125 us
  starting transfers between devices: 27.5 us -> 0 us
  between operations: 13.5 us -> 0.05 us
    all_to_all x2 -> x0, waiting for transfers between devices: 62.1 us -> none  [the longest x1 55.9 us: body(): lax.all_to_all(jnp.concatenate([rows, maps], axis=1), 'shard', split_axis...]
    pallas_call x1, Pallas kernels: 22.4 us -> 81.9 us  [exchange_rows(): pl.pallas_call(exchange_kernel, out_shape=[jax.ShapeDtypeStruct(*shape) f...]
    all_to_all x2 -> x0, starting transfers between devices: 27.4 us -> none  [the longest x1 14.5 us: body(): lax.all_to_all(jnp.concatenate([rows, maps], axis=1), 'shard', split_axis...]
    all_gather x1 -> x0, waiting for transfers between devices: 13.7 us -> none  [body(): table = lax.all_gather(item_table.T, 'rep', axis=0, tiled=True)]
    pallas_call x1, Pallas kernels: 20.9 us -> 23.9 us  [layer(): pl.pallas_call(layer_kernel, grid=(seq_dev,), out_shape=jax.ShapeDtypeStr...]
  transfers between devices with their start and end apart: 3 -> 0, of which waited for: 3 -> 0; matrix products, arithmetic and copies ran while one was open for 3% -> 0% of each run, Pallas kernels for 10% -> 0%
where the time goes in v2:
time: 131 us
  Pallas kernels  125 us (95%)
  other arithmetic  3.35 us (3%)
  local copies, waits for them, and re-layouts  2.7 us (2%)
    pallas_call x1, Pallas kernels, exchange_rows(): pl.pallas_call(exchange_kernel, out_shape=[jax.ShapeDtypeStruct(*shape) f...  81.9 us
    pallas_call x1, Pallas kernels, layer(): pl.pallas_call(layer_kernel, grid=(seq_dev,), out_shape=jax.ShapeDtypeStr...  23.9 us
    pallas_call x1, Pallas kernels, plan_requests(): pl.pallas_call(plan_kernel, out_shape=jax.ShapeDtypeStruct((shards, 128),...  18.7 us
    sort x1, other arithmetic, body(): order = jnp.argsort(owners, stable=True)  3.19 us

profile of v2, /device:TPU:1, one launch (start us, length us, event | category | flops | bytes accessed | tf_op | source)
XLA Modules:
  0.0 130.6 jit_solution(15492263019666791750)
XLA Ops:
  0.0 0.0 copy-start
  0.0 0.0 copy-start.4
  0.0 0.0 copy-start.2
  0.0 0.0 copy-start.1
  0.0 0.6 copy-done
  0.7 0.7 dynamic-slice_bitcast_fusion.len_smem
  1.3 3.2 %sort.17 = (s32[128]{0:T(128)}, s32[128]{0:T(128)S(1)}) sort(s32[128]{0:T(128)} %bitcast.12, s32[128]{0:T(128)S(1)} %iota.4), dimensions={0}, to_apply=%region_0.0 | sort | flops 896 | bytes 2048 | tf_op jit(solution)/shard_map/jit(argsort)/sort | solution.py:492
  4.5 0.1 compare_select_fusion.2
  4.6 0.6 gather_fusion
  5.2 0.1 pad_add_fusion.info_ref
  5.3 18.7 %plan.1 = s32[64,128]{1,0:T(8,128)} custom-call(s32[2,1024]{1,0:T(2,128)} %ids_ref.1, s32[2]{0:T(128)} %dynamic-slice_bitcast_fusion.len_smem, s32[2,1024]{1,0:T(2,128)} %ids_ref.1, s32[4096,128]{1,0:T(8,128)} %bitcast.11), custom_call_target="tpu_custom_call" | custom-call | tf_op jit(solution)/shard_map/plan/pallas_call | solution.py:94
  24.0 0.0 copy-done.1
  24.1 0.0 copy-start.3
  24.1 0.8 copy-done.3
  24.8 81.9 %exchange.1 = (bf16[64,32,128]{2,1,0:T(8,128)(2,1)S(1)}, bf16[64,64,128]{2,1,0:T(8,128)(2,1)S(1)}, bf16[64,32,128]{2,1,0:T(8,128)(2,1)S(1)}, s32[64,2,128]{2,1,0:T(2,128)S(1)}) custom-call(s32[128]{0:T(128)S(1)} %get-tuple-element.10.order_ref, s32[64,1,128]{2,1,0:T(1,128)S(1)} %bitcast.10, bf16[64,8192]{1,0:T(8,128)(2,1)S(1)} %bitcast.9), custom_call_target="tpu_custom_call" | custom-call | tf_op jit(solution)/shard_map/exchange/pallas_call | solution.py:290
  106.7 0.0 copy-done.4
  106.7 0.0 copy-done.2
  106.7 23.9 %layer.1 = bf16[2,1024,256]{2,1,0:T(8,128)(2,1)} custom-call(s32[64,2,128]{2,1,0:T(2,128)S(1)} %get-tuple-element.11.maps_ref, s32[5]{0:T(128)S(1)} %pad_add_fusion.info_ref, bf16[64,32,128]{2,1,0:T(8,128)(2,1)S(1)} %get-tuple-element.12.own_ref, bf16[64,64,128]{2,1,0:T(8,128)(2,1)S(1)} %get-tuple-element.13.pair_ref, ...), custom_call_target="tpu_custom_call" | custom-call | tf_op jit(solution)/shard_map/layer/pallas_call | solution.py:458
  (2 shorter events, 0.0 us)
Async XLA Ops:
  0.0 0.7 copy-start
  0.0 106.7 %copy-start.4 = (bf16[256,256]{1,0:T(8,128)(2,1)S(1)}, bf16[256,256]{1,0:T(8,128)(2,1)}, u32[]{:S(2)}) copy-start(bf16[256,256]{1,0:T(8,128)(2,1)} %outw_ref.1) | copy-start | bytes 393220
  0.0 106.7 %copy-start.2 = (bf16[256,1024]{1,0:T(8,128)(2,1)S(1)}, bf16[256,1024]{1,0:T(8,128)(2,1)}, u32[]{:S(2)}) copy-start(bf16[256,1024]{1,0:T(8,128)(2,1)} %proj_ref.1) | copy-start | bytes 1572868
  0.0 24.0 %copy-start.1 = (bf16[8192,64]{0,1:T(8,128)(2,1)S(1)}, bf16[8192,64]{0,1:T(8,128)(2,1)}, u32[]{:S(2)}) copy-start(bf16[8192,64]{0,1:T(8,128)(2,1)} %param.11) | copy-start | bytes 3145732
  24.1 0.8 copy-start.3

commit v3 on v2

--- a/solution.py
+++ b/solution.py
@@ -30,92 +30,89 @@
     return lax.dot_general(left, right, (((0,), (0,)), ((), ())), preferred_element_type=F32)
 
 
-def plan_kernel(ids_smem, len_smem, ids_ref, home_ref, out_ref, stage):
+def plan_order(owner_ref):
+    size = owner_ref.shape[1]
+    row = owner_ref[...]
+    col = column_of(row, size)
+    sub = lax.broadcasted_iota(I32, (size, size), 0)
+    lane = lax.broadcasted_iota(I32, (size, size), 1)
+    keyed = row.astype(F32)
+    before = (col < keyed) | ((col == keyed) & (sub < lane))
+    rank = jnp.sum(jnp.where(before, 1.0, 0.0), axis=0, keepdims=True)
+    found = jnp.where(rank == sub.astype(F32), lane.astype(F32), 0.0)
+    at = jnp.sum(found, axis=1, keepdims=True)
+    return jnp.sum(jnp.where(sub == lane, at, 0.0), axis=0, keepdims=True).astype(I32) & (size - 1)
+
+
+def plan_fetch(ids_smem, home, stage):
+    def fetch(c, carry):
+        for i in range(128):
+            line = lax.shift_right_logical(ids_smem[c, i], 7)
+            stage[c, pl.ds(i, 1), :] = home[pl.ds(line, 1), :]
+        return carry
+
+    lax.fori_loop(0, ids_smem.shape[0], fetch, 0)
+
+
+def plan_requests(seq, length, ids_ref, stage, shards, rows_dev):
     seq_len = ids_ref.shape[1]
-    shards = out_ref.shape[0]
-    rows_dev = home_ref.shape[0] * 128 // shards
-    step = 32
-
-    for seq in range(2):
-
-        def fetch(c, carry):
-            for i in range(step):
-                t = c * step + i
-                row = ids_smem[seq, t] // 128
-                stage[pl.ds(seq * seq_len + t, 1), :] = home_ref[pl.ds(row, 1), :]
-            return carry
-
-        lax.fori_loop(0, seq_len // step, fetch, 0)
-
-    place = lax.broadcasted_iota(I32, (seq_len, 1), 0)
-    lane = lax.broadcasted_iota(I32, (seq_len, 128), 1)
-    lane_k = lax.broadcasted_iota(I32, (seq_len, shards), 1)
-    below = (
-        lax.broadcasted_iota(I32, (128, 128), 1) < lax.broadcasted_iota(I32, (128, 128), 0)
-    ).astype(BF16)
-    own = ((place // 16) == lane_k).astype(BF16)
-    result = jnp.zeros((shards, 128), F32)
-    for seq in range(2):
-        ids = column_of(ids_ref[seq : seq + 1, :], seq_len).astype(I32)
-        picked = jnp.where(
-            (ids & 127) == lane, stage[pl.ds(seq * seq_len, seq_len), :].astype(F32), 0.0
+    chunk = seq_len // shards
+    shift = rows_dev.bit_length() - 1
+    place = lax.broadcasted_iota(I32, (128, 1), 0)
+    lane = lax.broadcasted_iota(I32, (128, 128), 1)
+    lane_k = lax.broadcasted_iota(I32, (128, shards), 1)
+    sub = lax.broadcasted_iota(I32, (128, 128), 0)
+    below = (lane < sub).astype(BF16)
+    eye = lane == sub
+    carry = jnp.zeros((1, shards), F32)
+    lefts, rights = [], []
+    owns, slots = [], []
+    for b in range(seq_len // 128):
+        ids = jnp.sum(
+            jnp.where(eye, (ids_ref[seq : seq + 1, b * 128 : (b + 1) * 128] & 127).astype(F32), 0.0),
+            axis=1,
+            keepdims=True,
         )
-        home = jnp.sum(picked, axis=1, keepdims=True).astype(I32)
-        target = home // rows_dev
+        lines = stage[seq * (seq_len // 128) + b].astype(F32)
+        home = jnp.sum(
+            jnp.where(ids == lane.astype(F32), lines, 0.0), axis=1, keepdims=True
+        ).astype(I32)
+        at = place + b * 128
+        target = jnp.where(at < length, lax.shift_right_logical(home, shift), shards)
         row = home & (rows_dev - 1)
-        live = place < len_smem[seq]
-        onehot = jnp.where((target == lane_k) & live, 1.0, 0.0)
+        onehot = jnp.where(target == lane_k, 1.0, 0.0)
         onehot16 = onehot.astype(BF16)
-        carry = jnp.zeros((1, shards), F32)
-        ranks = []
-        for b in range(seq_len // 128):
-            part = onehot[b * 128 : (b + 1) * 128]
-            before = jnp.dot(below, part.astype(BF16), preferred_element_type=F32) + carry
-            ranks.append(jnp.sum(before * part, axis=1, keepdims=True))
-            carry = carry + jnp.sum(part, axis=0, keepdims=True)
-        rank = jnp.concatenate(ranks, axis=0).astype(I32)
-        at_rank = lane == rank + seq * CAP
-        count = jnp.where(lane == 96 + seq, 1.0, 0.0)
-        high = jnp.where(at_rank, (row & ~127).astype(F32), count)
-        low = jnp.where(at_rank, (row & 127).astype(F32), 0.0)
-        result = result + contract_rows(onehot16, high.astype(BF16))
-        result = result + contract_rows(onehot16, low.astype(BF16))
-        slot = jnp.where(live, target * CAP + rank, 0)
-        at_place = lane == (place & 15) + (64 + seq * 16)
-        high = jnp.where(at_place, (slot & ~127).astype(F32), 0.0)
-        low = jnp.where(at_place, (slot & 127).astype(F32), 0.0)
-        result = result + contract_rows(own, high.astype(BF16))
-        result = result + contract_rows(own, low.astype(BF16))
-    out_ref[...] = result.astype(I32)
-
-
-def plan_requests(item_ids, lengths, row_home, shards):
-    seq_dev, seq_len = item_ids.shape
-    return pl.pallas_call(
-        plan_kernel,
-        out_shape=jax.ShapeDtypeStruct((shards, 128), I32),
-        in_specs=[
-            pl.BlockSpec(memory_space=pltpu.SMEM),
-            pl.BlockSpec(memory_space=pltpu.SMEM),
-            pl.BlockSpec(memory_space=pltpu.VMEM),
-            pl.BlockSpec(memory_space=pltpu.VMEM),
-        ],
-        out_specs=pl.BlockSpec(memory_space=pltpu.VMEM),
-        scratch_shapes=[pltpu.VMEM((seq_dev * seq_len, 128), I32)],
-        name="plan",
-    )(item_ids, lengths, item_ids, row_home.reshape(-1, 128))
+        before = jnp.dot(below, onehot16, preferred_element_type=F32) + carry
+        rank = jnp.sum(before * onehot, axis=1, keepdims=True)
+        carry = carry + jnp.sum(onehot, axis=0, keepdims=True)
+        at_rank = lane.astype(F32) == rank
+        lefts += [onehot16, onehot16]
+        rights.append(jnp.where(at_rank, (row & ~127).astype(F32), 0.0).astype(BF16))
+        rights.append(jnp.where(at_rank, (row & 127).astype(F32), 0.0).astype(BF16))
+        slot = jnp.where(at < length, target * CAP + rank.astype(I32), 0)
+        own = jnp.where(at // chunk == lane_k, 1.0, 0.0).astype(BF16)
+        at_place = lane == lax.rem(at, chunk) + CAP
+        lefts += [own, own]
+        rights.append(jnp.where(at_place, (slot & ~127).astype(F32), 0.0).astype(BF16))
+        rights.append(jnp.where(at_place, (slot & 127).astype(F32), 0.0).astype(BF16))
+    result = contract_rows(jnp.concatenate(lefts, axis=0), jnp.concatenate(rights, axis=0))
+    lanes = lax.broadcasted_iota(I32, (shards, 128), 1)
+    result = result.astype(I32)
+    result = jnp.where(lanes < CAP, result & (rows_dev - 1), result & (shards * CAP - 1))
+    return jnp.where(lanes == CAP + 16, length, result)
 
 
 def exchange_kernel(
-    order_ref, asked_ref, table_ref,
+    ids_smem, len_smem, ids_ref, owner_ref, home_ref, table_ref,
     own_got, pair_got, far_got, maps_got,
-    asked_all, asked_smem, table_in, left_in, right_in, far_in,
+    home_in, lines, asked_ref, asked_all, asked_smem, order_in, order_ref, table_in, left_in, right_in, far_in,
     own_rows, pair_rows, far_rows, stage,
     own_out, pair_out, far_out, maps_out,
     local_sem, asked_send, asked_recv, side_send, side_recv, row_send, row_recv,
 ):
-    shards = asked_ref.shape[0]
+    shards = own_got.shape[0]
     reps = 4
+    seq_dev, seq_len = ids_ref.shape
     cols, rows_dev = table_ref.shape
     me = lax.axis_index("shard")
     rep = lax.axis_index("rep")
@@ -124,6 +121,8 @@
     chunk = min(256, rows_dev)
 
     load = pltpu.make_async_copy(table_ref, table_in, local_sem.at[0])
+    load_home = pltpu.make_async_copy(home_ref, home_in, local_sem.at[1])
+    load_home.start()
     load.start()
     barrier = pltpu.get_barrier_semaphore()
 
@@ -155,6 +154,9 @@
 
         lax.fori_loop(0, rows_dev // chunk, one, 0)
 
+    order_in[...] = plan_order(owner_ref)
+    load_home.wait()
+    plan_fetch(ids_smem, home_in, lines)
     load.wait()
     pl.semaphore_wait(barrier, shards + 1)
 
@@ -178,6 +180,14 @@
             device_id_type=pl.DeviceIdType.MESH,
         )
 
+    to_right = side_copy(table_in, left_in, 0, right)
+    to_left = side_copy(table_in, right_in, 1, left)
+    to_right.start()
+    to_left.start()
+    for seq in range(seq_dev):
+        length = len_smem[0, me * seq_dev + seq]
+        asked_ref[:, seq, :] = plan_requests(seq, length, ids_ref, lines, shards, rows_dev)
+
     def ask(i, carry):
         peer = lax.rem(me + i, shards)
         shard_copy(
@@ -186,17 +196,16 @@
         return carry
 
     lax.fori_loop(1, shards, ask, 0)
-    keep = pltpu.make_async_copy(asked_ref.at[me], asked_all.at[me], local_sem.at[1])
+    keep = pltpu.make_async_copy(asked_ref.at[me], asked_all.at[me], local_sem.at[2])
     keep.start()
-    to_right = side_copy(table_in, left_in, 0, right)
-    to_left = side_copy(table_in, right_in, 1, left)
-    to_right.start()
-    to_left.start()
+    spill_order = pltpu.make_async_copy(order_in, order_ref, local_sem.at[3])
+    spill_order.start()
     turn(table_in, table_in, own_rows)
     keep.wait()
+    spill_order.wait()
     others = pl.ds(0, shards - 1)
     shard_copy(asked_ref.at[others], asked_all.at[others], asked_send, asked_recv, me).wait()
-    spill = pltpu.make_async_copy(asked_all, asked_smem, local_sem.at[2])
+    spill = pltpu.make_async_copy(asked_all, asked_smem, local_sem.at[4])
     spill.start()
     spill.wait()
 
@@ -206,34 +215,33 @@
         shard_copy(out.at[peer], got.at[me], row_send.at[kind], row_recv.at[kind], peer).start()
 
     def finish(out, got, kind):
-        local = pltpu.make_async_copy(out.at[me], got.at[me], local_sem.at[3 + kind])
+        local = pltpu.make_async_copy(out.at[me], got.at[me], local_sem.at[5 + kind])
         local.start()
         local.wait()
 
     def sweep(pick, out, got, kind, paired, extra=None):
         def owner(i, carry):
             peer = lax.rem(me + i + 1, shards)
-            sources = []
-            offsets = []
-            for q in range(2):
-                hist = order_ref[2 * peer + q]
-                sources.append(hist // 2)
-                offsets.append(lax.rem(hist, 2) * CAP)
+            hists = [order_ref[0, 2 * peer + q] for q in range(2)]
             if extra is not None:
                 for q in range(2):
-                    extra[peer, pl.ds(q, 1), :] = asked_all[sources[q]]
+                    line = asked_all[lax.shift_right_logical(hists[q], 1)]
+                    odd = lax.rem(hists[q], 2) == 1
+                    extra[peer, pl.ds(q, 1), :] = jnp.where(odd, line[1:2], line[0:1])
+            sources = [lax.shift_right_logical(hist, 1) for hist in hists]
+            halves = [hist & 1 for hist in hists]
             slot = lax.rem(i, 2)
             if paired:
                 for j in range(CAP):
-                    one = pick[pl.ds(asked_smem[sources[0], 0, offsets[0] + j], 1), :]
-                    two = pick[pl.ds(asked_smem[sources[1], 0, offsets[1] + j], 1), :]
+                    one = pick[pl.ds(asked_smem[sources[0], halves[0], j], 1), :]
+                    two = pick[pl.ds(asked_smem[sources[1], halves[1], j], 1), :]
                     stage[slot, pl.ds(j, 1), :] = jnp.where(first_half, one, two)
                 out[peer] = stage[slot, :CAP, :].astype(BF16)
             else:
                 for q in range(2):
                     for j in range(CAP):
                         stage[slot, pl.ds(q * CAP + j, 1), :] = pick[
-                            pl.ds(asked_smem[sources[q], 0, offsets[q] + j], 1), :
+                            pl.ds(asked_smem[sources[q], halves[q], j], 1), :
                         ]
                 out[peer] = stage[slot].astype(BF16)
 
@@ -276,29 +284,34 @@
         ).wait()
 
 
-def exchange_rows(order, asked, table):
-    shards = asked.shape[0]
+def exchange_rows(item_ids, lengths, owners, row_home, table, shards):
     cols, rows_dev = table.shape
+    seq_dev, seq_len = item_ids.shape
     wide = 2 * cols
     any_space = pl.BlockSpec(memory_space=pl.ANY)
+    smem_space = pl.BlockSpec(memory_space=pltpu.SMEM)
+    vmem_space = pl.BlockSpec(memory_space=pltpu.VMEM)
+    lines = seq_dev * seq_len // 128
     shapes = (
         ((shards, CAP, wide), BF16),
         ((shards, 2 * CAP, wide), BF16),
         ((shards, CAP, wide), BF16),
-        ((shards, 2, 128), I32),
+        ((shards, seq_dev, 128), I32),
     )
+    home = row_home.reshape(-1, 128)
     return pl.pallas_call(
         exchange_kernel,
         out_shape=[jax.ShapeDtypeStruct(*shape) for shape in shapes],
-        in_specs=[
-            pl.BlockSpec(memory_space=pltpu.SMEM),
-            pl.BlockSpec(memory_space=pltpu.VMEM),
-            any_space,
-        ],
+        in_specs=[smem_space, smem_space, vmem_space, vmem_space, any_space, any_space],
         out_specs=[any_space] * 4,
         scratch_shapes=[
-            pltpu.VMEM((shards, 1, 128), I32),
-            pltpu.SMEM((shards, 1, 128), I32),
+            pltpu.VMEM(home.shape, I32),
+            pltpu.VMEM((lines, 128, 128), I32),
+            pltpu.VMEM((shards, seq_dev, 128), I32),
+            pltpu.VMEM((shards, seq_dev, 128), I32),
+            pltpu.SMEM((shards, seq_dev, 128), I32),
+            pltpu.VMEM(owners.shape, I32),
+            pltpu.SMEM(owners.shape, I32),
             pltpu.VMEM((cols, rows_dev), BF16),
             pltpu.VMEM((cols, rows_dev), BF16),
             pltpu.VMEM((cols, rows_dev), BF16),
@@ -308,7 +321,7 @@
             pltpu.VMEM((rows_dev, wide), F32),
             pltpu.VMEM((2, 2 * CAP, wide), F32),
             *[pltpu.VMEM(*shape) for shape in shapes],
-            pltpu.SemaphoreType.DMA((7,)),
+            pltpu.SemaphoreType.DMA((9,)),
             pltpu.SemaphoreType.DMA,
             pltpu.SemaphoreType.DMA,
             pltpu.SemaphoreType.DMA((4,)),
@@ -320,7 +333,7 @@
             collective_id=0, has_side_effects=True, vmem_limit_bytes=40 * 1024 * 1024
         ),
         name="exchange",
-    )(order, asked.reshape(shards, 1, 128), table)
+    )(item_ids.reshape(lines, 128), lengths, item_ids, owners, home, table)
 
 
 def normed_rows(values):
@@ -334,15 +347,14 @@
 
 
 def layer_kernel(
-    maps_ref, info_ref, own_ref, pair_ref, far_ref, proj_ref, outw_ref, mixed_ref,
+    maps_ref, own_ref, pair_ref, far_ref, proj_ref, outw_ref, mixed_ref,
     flat, emb, gates, vals, quer, keys, att,
 ):
     seq = pl.program_id(0)
     seq_len, width = mixed_ref.shape[1:]
     head = width // HEADS
-    length = info_ref[seq]
-    offset = 64 + 16 * info_ref[2 + seq]
-    rep = info_ref[4]
+    length = maps_ref[0, seq, CAP + 16]
+    rep = lax.axis_index("rep")
     shards, cap = own_ref.shape[:2]
     side = width // 4
     group = 8
@@ -373,9 +385,7 @@
                 for tile in range(2):
                     low = parts[names[(2 * tile - r) % 4]][0]
                     high = parts[names[(2 * tile + 1 - r) % 4]][1]
-                    flat[pl.ds(at, rows), tile * 2 * side : (tile + 1) * 2 * side] = jnp.where(
-                        first_half, low, high
-                    )
+                    flat[tile, pl.ds(at, rows), :] = jnp.where(first_half, low, high)
                 return carry
 
             lax.fori_loop(0, shards // group, place_blocks, 0)
@@ -384,20 +394,24 @@
 
     def fetch(c, carry):
         for i in range(unroll):
-            t = c * unroll + i
-            slot = maps_ref[c, seq, offset + i]
-            emb[pl.ds(t, 1), :] = flat[pl.ds(slot, 1), :]
+            slot = maps_ref[c, seq, CAP + i]
+            for tile in range(2):
+                emb[tile, c, pl.ds(i, 1), :] = flat[tile, pl.ds(slot, 1), :]
         return carry
 
     lax.fori_loop(0, (length + unroll - 1) // unroll, fetch, 0)
+
+    def rows_of(b):
+        span = pl.ds(b * (BLOCK // unroll), BLOCK // unroll)
+        return jnp.concatenate([emb[t, span].reshape(BLOCK, 2 * side) for t in range(2)], axis=1)
+
     blocks = (length + BLOCK - 1) // BLOCK
     place = lax.broadcasted_iota(I32, (BLOCK, 1), 0)
 
     def project(b, carry):
         at = pl.multiple_of(b * BLOCK, BLOCK)
         span = pl.ds(at, BLOCK)
-        rows = jnp.where(place + at < length, emb[span, :], 0.0)
-        emb[span, :] = rows
+        rows = jnp.where(place + at < length, rows_of(b), 0.0)
         normed = normed_rows(rows).astype(BF16)
         for part, ref in enumerate((gates, vals, quer, keys)):
             raw = jnp.dot(
@@ -439,7 +453,7 @@
             lax.fori_loop(0, HEADS, attend, 0)
             whole = jnp.concatenate([att[h] for h in range(HEADS)], axis=1) * inverse
             gated = (normed_rows(whole) * gates[b * BLOCK : reach, :].astype(F32)).astype(BF16)
-            mixed = emb[b * BLOCK : reach, :] + jnp.dot(
+            mixed = rows_of(b) + jnp.dot(
                 gated, outw_ref[...], preferred_element_type=F32
             )
             live = place + b * BLOCK < length
@@ -450,7 +464,7 @@
             mixed_ref[0, b * BLOCK : (b + 1) * BLOCK, :] = jnp.zeros((BLOCK, width), BF16)
 
 
-def layer(maps, info, own, pair, far, proj_weight, out_weight, seq_len):
+def layer(maps, own, pair, far, proj_weight, out_weight, seq_len):
     shards, cap, wide = own.shape
     seq_dev = 2
     width = proj_weight.shape[0]
@@ -461,7 +475,6 @@
         out_shape=jax.ShapeDtypeStruct((seq_dev, seq_len, width), BF16),
         in_specs=[
             pl.BlockSpec(memory_space=pltpu.SMEM),
-            pl.BlockSpec(memory_space=pltpu.SMEM),
             pl.BlockSpec((shards, cap, wide), lambda i: (0, 0, 0)),
             pl.BlockSpec((shards, cap, wide), lambda i: (0, i, 0)),
             pl.BlockSpec((shards, cap, wide), lambda i: (0, 0, 0)),
@@ -470,8 +483,8 @@
         ],
         out_specs=pl.BlockSpec((1, seq_len, width), lambda i: (i, 0, 0)),
         scratch_shapes=[
-            pltpu.VMEM((shards * cap, width), F32),
-            pltpu.VMEM((seq_len, width), F32),
+            pltpu.VMEM((2, shards * cap, wide), F32),
+            pltpu.VMEM((2, seq_len // 16, 16, wide), F32),
             pltpu.VMEM((seq_len, width), BF16),
             pltpu.VMEM((HEADS, seq_len, head), BF16),
             pltpu.VMEM((HEADS, seq_len, head), BF16),
@@ -480,23 +493,16 @@
         ],
         compiler_params=pltpu.CompilerParams(vmem_limit_bytes=48 * 1024 * 1024),
         name="layer",
-    )(maps, info, own, pair, far, proj_weight, out_weight)
+    )(maps, own, pair, far, proj_weight, out_weight)
 
 
 def body(item_ids, seq_lengths, seq_owner, row_home, item_table, proj_weight, out_weight):
     shards = lax.axis_size("shard")
-    me = lax.axis_index("shard")
-    seq_dev, seq_len = item_ids.shape
-    owners = seq_owner[0]
-    lengths = seq_lengths[0]
-    order = jnp.argsort(owners, stable=True)
-    mine = lax.dynamic_slice_in_dim(order, me * seq_dev, seq_dev)
-    held = lax.dynamic_slice_in_dim(lengths, me * seq_dev, seq_dev)
-    asked = plan_requests(item_ids, held, row_home, shards)
-    own, pair, far, maps = exchange_rows(order, asked, item_table.T)
-    rep = lax.axis_index("rep").reshape(1)
-    info = jnp.concatenate([lengths[mine], mine % 2, rep])
-    return layer(maps, info, own, pair, far, proj_weight, out_weight, seq_len)
+    seq_len = item_ids.shape[1]
+    own, pair, far, maps = exchange_rows(
+        item_ids, seq_lengths, seq_owner, row_home, item_table.T, shards
+    )
+    return layer(maps, own, pair, far, proj_weight, out_weight, seq_len)
 
 
 def solution(mesh):

time: 131 us -> 106 us (0.81)
  Pallas kernels: 125 us -> 101 us
  other arithmetic: 3.35 us -> 0 us
  local copies, waits for them, and re-layouts: 2.7 us -> 5.53 us
    pallas_call x1 -> x0, Pallas kernels: 18.7 us -> none  [plan_requests(): pl.pallas_call(plan_kernel, out_shape=jax.ShapeDtypeStruct((shards, 128),...]
    pallas_call x1, Pallas kernels: 23.9 us -> 19.7 us  [layer(): pl.pallas_call(layer_kernel, grid=(seq_dev,), out_shape=jax.ShapeDtypeStr...]
    unnamed x10 -> x14, local copies, waits for them, and re-layouts: 1.4 us -> 4.83 us
    sort x1 -> x0, other arithmetic: 3.19 us -> none  [body(): order = jnp.argsort(owners, stable=True)]
where the time goes in v3:
time: 106 us
  Pallas kernels  101 us (95%)
  local copies, waits for them, and re-layouts  5.53 us (5%)
    pallas_call x1, Pallas kernels, exchange_rows(): pl.pallas_call(exchange_kernel, out_shape=[jax.ShapeDtypeStruct(*shape) f...  80.8 us
    pallas_call x1, Pallas kernels, layer(): pl.pallas_call(layer_kernel, grid=(seq_dev,), out_shape=jax.ShapeDtypeStr...  19.7 us
    unnamed x14, local copies, waits for them, and re-layouts  4.83 us

profile of v3, /device:TPU:1, one launch (start us, length us, event | category | flops | bytes accessed | tf_op | source)
XLA Modules:
  0.0 106.1 jit_solution(4600714776763768238)
XLA Ops:
  0.0 0.7 reshape.6.ids_smem
  0.7 0.0 copy-start
  0.7 1.6 %copy-done = s32[524288]{0:T(1024)S(1)} copy-done((s32[524288]{0:T(1024)S(1)}, s32[524288]{0:T(1024)}, u32[]{:S(2)}) %copy-start) | copy-done | bytes 2097176
  2.3 0.0 copy-start.1
  2.3 1.2 %copy-done.1 = bf16[8192,64]{0,1:T(8,128)(2,1)S(1)} copy-done((bf16[8192,64]{0,1:T(8,128)(2,1)S(1)}, bf16[8192,64]{0,1:T(8,128)(2,1)}, u32[]{:S(2)}) %copy-start.1) | copy-done | bytes 1048600
  3.5 0.0 copy-start.4
  3.5 0.7 copy-done.4
  4.2 0.0 copy-start.5
  4.2 0.7 copy-done.5
  4.9 0.0 copy-start.6
  4.9 0.7 copy-done.6
  5.5 0.0 copy-start.2
  5.5 0.0 copy-start.3
  5.5 80.8 %exchange.1 = (bf16[64,32,128]{2,1,0:T(8,128)(2,1)S(1)}, bf16[64,64,128]{2,1,0:T(8,128)(2,1)S(1)}, bf16[64,32,128]{2,1,0:T(8,128)(2,1)S(1)}, s32[64,2,128]{2,1,0:T(2,128)S(1)}) custom-call(s32[16,128]{1,0:T(8,128)S(1)} %reshape.6.ids_smem, s32[1,128]{1,0:T(1,128)S(1)} %copy-done.5, s32[2,1024]{1,0:T(2,128)S(1)} %copy-done.4, s32[1,128]{1,0:T(1,128)S(1)} %copy-done.6, ...), custom_call_target="tpu_custom_call" | custom-call | tf_op jit(solution)/shard_map/exchange/pallas_call | solution.py:302
  86.4 0.0 copy-done.2
  86.4 0.0 copy-done.3
  86.4 19.7 %layer.1 = bf16[2,1024,256]{2,1,0:T(8,128)(2,1)} custom-call(s32[64,2,128]{2,1,0:T(2,128)S(1)} %get-tuple-element.9.maps_ref, bf16[64,32,128]{2,1,0:T(8,128)(2,1)S(1)} %get-tuple-element.10.own_ref, bf16[64,64,128]{2,1,0:T(8,128)(2,1)S(1)} %get-tuple-element.11.pair_ref, bf16[64,32,128]{2,1,0:T(8,128)(2,1)S(1)} %get-tuple-element.12.far_ref, ...), custom_call_target="tpu_custom_call" | custom-call | tf_op jit(solution)/shard_map/layer/pallas_call | solution.py:472
Async XLA Ops:
  0.7 1.6 %copy-start = (s32[524288]{0:T(1024)S(1)}, s32[524288]{0:T(1024)}, u32[]{:S(2)}) copy-start(s32[524288]{0:T(1024)} %param.10) | copy-start | bytes 6291460
  2.3 1.2 %copy-start.1 = (bf16[8192,64]{0,1:T(8,128)(2,1)S(1)}, bf16[8192,64]{0,1:T(8,128)(2,1)}, u32[]{:S(2)}) copy-start(bf16[8192,64]{0,1:T(8,128)(2,1)} %param.11) | copy-start | bytes 3145732
  3.5 0.7 copy-start.4
  4.2 0.7 copy-start.5
  4.9 0.7 copy-start.6
  5.5 80.9 %copy-start.2 = (bf16[256,1024]{1,0:T(8,128)(2,1)S(1)}, bf16[256,1024]{1,0:T(8,128)(2,1)}, u32[]{:S(2)}) copy-start(bf16[256,1024]{1,0:T(8,128)(2,1)} %proj_ref.1) | copy-start | bytes 1572868
  5.5 80.9 %copy-start.3 = (bf16[256,256]{1,0:T(8,128)(2,1)S(1)}, bf16[256,256]{1,0:T(8,128)(2,1)}, u32[]{:S(2)}) copy-start(bf16[256,256]{1,0:T(8,128)(2,1)} %outw_ref.1) | copy-start | bytes 393220

commit v4 on v3

--- a/solution.py
+++ b/solution.py
@@ -103,9 +103,9 @@
 
 
 def exchange_kernel(
-    ids_smem, len_smem, ids_ref, owner_ref, home_ref, table_ref,
+    ids_hbm, len_hbm, owner_hbm, home_ref, table_ref,
     own_got, pair_got, far_got, maps_got,
-    home_in, lines, asked_ref, asked_all, asked_smem, order_in, order_ref, table_in, left_in, right_in, far_in,
+    ids_ref, ids_lines, ids_smem, len_smem, owner_ref, home_in, lines, asked_ref, asked_all, asked_smem, order_in, order_ref, table_in, left_in, right_in, far_in,
     own_rows, pair_rows, far_rows, stage,
     own_out, pair_out, far_out, maps_out,
     local_sem, asked_send, asked_recv, side_send, side_recv, row_send, row_recv,
@@ -122,9 +122,30 @@
 
     load = pltpu.make_async_copy(table_ref, table_in, local_sem.at[0])
     load_home = pltpu.make_async_copy(home_ref, home_in, local_sem.at[1])
+    load_ids = pltpu.make_async_copy(ids_hbm, ids_ref, local_sem.at[2])
+    load_owner = pltpu.make_async_copy(owner_hbm, owner_ref, local_sem.at[3])
+    load_len = pltpu.make_async_copy(len_hbm, len_smem, local_sem.at[4])
+    load_ids.start()
+    load_owner.start()
+    load_len.start()
     load_home.start()
     load.start()
     barrier = pltpu.get_barrier_semaphore()
+
+    depth = min(8, shards // 2)
+    spread = shards // (2 * depth)
+
+    def toward(i, size):
+        step = (i + 1) // 2
+        return lax.rem(size // 2 + step * (2 * lax.rem(i, 2) - 1) + size, size)
+
+    def peer_at(i):
+        dz = toward(i // (2 * spread), depth)
+        dx = toward(lax.rem(i // 2, spread), spread)
+        core = lax.rem(lax.rem(me, 2) + 1 + lax.rem(i, 2), 2)
+        z = lax.rem(me // 2 + dz, depth)
+        x = lax.rem(me // (2 * depth) + dx, spread)
+        return (x * depth + z) * 2 + core
 
     def greet(i, carry):
         peer = lax.rem(me + i, shards)
@@ -154,9 +175,19 @@
 
         lax.fori_loop(0, rows_dev // chunk, one, 0)
 
+    load_ids.wait()
+    for seq in range(seq_dev):
+        for b in range(seq_len // 128):
+            at = seq * (seq_len // 128) + b
+            ids_lines[at : at + 1, :] = ids_ref[seq : seq + 1, b * 128 : (b + 1) * 128]
+    load_owner.wait()
     order_in[...] = plan_order(owner_ref)
+    spill_ids = pltpu.make_async_copy(ids_lines, ids_smem, local_sem.at[5])
+    spill_ids.start()
+    spill_ids.wait()
     load_home.wait()
     plan_fetch(ids_smem, home_in, lines)
+    load_len.wait()
     load.wait()
     pl.semaphore_wait(barrier, shards + 1)
 
@@ -189,23 +220,23 @@
         asked_ref[:, seq, :] = plan_requests(seq, length, ids_ref, lines, shards, rows_dev)
 
     def ask(i, carry):
-        peer = lax.rem(me + i, shards)
+        peer = peer_at(i)
         shard_copy(
             asked_ref.at[peer], asked_all.at[me], asked_send, asked_recv, peer
         ).start()
         return carry
 
-    lax.fori_loop(1, shards, ask, 0)
-    keep = pltpu.make_async_copy(asked_ref.at[me], asked_all.at[me], local_sem.at[2])
+    lax.fori_loop(0, shards - 1, ask, 0)
+    keep = pltpu.make_async_copy(asked_ref.at[me], asked_all.at[me], local_sem.at[6])
     keep.start()
-    spill_order = pltpu.make_async_copy(order_in, order_ref, local_sem.at[3])
+    spill_order = pltpu.make_async_copy(order_in, order_ref, local_sem.at[7])
     spill_order.start()
     turn(table_in, table_in, own_rows)
     keep.wait()
     spill_order.wait()
     others = pl.ds(0, shards - 1)
     shard_copy(asked_ref.at[others], asked_all.at[others], asked_send, asked_recv, me).wait()
-    spill = pltpu.make_async_copy(asked_all, asked_smem, local_sem.at[4])
+    spill = pltpu.make_async_copy(asked_all, asked_smem, local_sem.at[8])
     spill.start()
     spill.wait()
 
@@ -214,14 +245,14 @@
     def send_to(out, got, kind, peer):
         shard_copy(out.at[peer], got.at[me], row_send.at[kind], row_recv.at[kind], peer).start()
 
-    def finish(out, got, kind):
-        local = pltpu.make_async_copy(out.at[me], got.at[me], local_sem.at[5 + kind])
+    def stay(out, got, kind):
+        local = pltpu.make_async_copy(out.at[me], got.at[me], local_sem.at[9 + kind])
         local.start()
-        local.wait()
+        return local
 
     def sweep(pick, out, got, kind, paired, extra=None):
         def owner(i, carry):
-            peer = lax.rem(me + i + 1, shards)
+            peer = peer_at(i)
             hists = [order_ref[0, 2 * peer + q] for q in range(2)]
             if extra is not None:
                 for q in range(2):
@@ -247,7 +278,7 @@
 
             @pl.when(i > 0)
             def _():
-                before = lax.rem(me + i, shards)
+                before = peer_at(i - 1)
                 send_to(out, got, kind, before)
                 if extra is not None:
                     send_to(extra, maps_got, 3, before)
@@ -265,23 +296,24 @@
     on_right.start()
     on_left.start()
     turn(left_in, right_in, pair_rows)
+    stays = [stay(own_out, own_got, 0), stay(maps_out, maps_got, 3)]
     sweep(pair_rows, pair_out, pair_got, 1, False)
     on_right.wait_recv()
     on_left.wait_recv()
     turn(far_in, far_in, far_rows)
+    stays.append(stay(pair_out, pair_got, 1))
     sweep(far_rows, far_out, far_got, 2, True)
-    for kind, (out, got) in enumerate(
-        ((own_out, own_got), (pair_out, pair_got), (far_out, far_got), (maps_out, maps_got))
-    ):
-        finish(out, got, kind)
     for copy in (to_right, to_left, on_right, on_left):
         copy.wait_send()
+    stays.append(stay(far_out, far_got, 2))
     for kind, (out, got) in enumerate(
         ((own_out, own_got), (pair_out, pair_got), (far_out, far_got), (maps_out, maps_got))
     ):
         shard_copy(
             out.at[others], got.at[others], row_send.at[kind], row_recv.at[kind], me
         ).wait()
+    for local in stays:
+        local.wait()
 
 
 def exchange_rows(item_ids, lengths, owners, row_home, table, shards):
@@ -289,8 +321,7 @@
     seq_dev, seq_len = item_ids.shape
     wide = 2 * cols
     any_space = pl.BlockSpec(memory_space=pl.ANY)
-    smem_space = pl.BlockSpec(memory_space=pltpu.SMEM)
-    vmem_space = pl.BlockSpec(memory_space=pltpu.VMEM)
+    hbm_space = pl.BlockSpec(memory_space=pltpu.HBM)
     lines = seq_dev * seq_len // 128
     shapes = (
         ((shards, CAP, wide), BF16),
@@ -302,9 +333,14 @@
     return pl.pallas_call(
         exchange_kernel,
         out_shape=[jax.ShapeDtypeStruct(*shape) for shape in shapes],
-        in_specs=[smem_space, smem_space, vmem_space, vmem_space, any_space, any_space],
+        in_specs=[hbm_space] * 5,
         out_specs=[any_space] * 4,
         scratch_shapes=[
+            pltpu.VMEM(item_ids.shape, I32),
+            pltpu.VMEM((lines, 128), I32),
+            pltpu.SMEM((lines, 128), I32),
+            pltpu.SMEM(lengths.shape, I32),
+            pltpu.VMEM(owners.shape, I32),
             pltpu.VMEM(home.shape, I32),
             pltpu.VMEM((lines, 128, 128), I32),
             pltpu.VMEM((shards, seq_dev, 128), I32),
@@ -321,7 +357,7 @@
             pltpu.VMEM((rows_dev, wide), F32),
             pltpu.VMEM((2, 2 * CAP, wide), F32),
             *[pltpu.VMEM(*shape) for shape in shapes],
-            pltpu.SemaphoreType.DMA((9,)),
+            pltpu.SemaphoreType.DMA((13,)),
             pltpu.SemaphoreType.DMA,
             pltpu.SemaphoreType.DMA,
             pltpu.SemaphoreType.DMA((4,)),
@@ -330,10 +366,10 @@
             pltpu.SemaphoreType.DMA((4,)),
         ],
         compiler_params=pltpu.CompilerParams(
-            collective_id=0, has_side_effects=True, vmem_limit_bytes=40 * 1024 * 1024
+            collective_id=0, has_side_effects=True, vmem_limit_bytes=60 * 1024 * 1024
         ),
         name="exchange",
-    )(item_ids.reshape(lines, 128), lengths, item_ids, owners, home, table)
+    )(item_ids, lengths, owners, home, table)
 
 
 def normed_rows(values):
@@ -347,11 +383,50 @@
 
 
 def layer_kernel(
-    maps_ref, own_ref, pair_ref, far_ref, proj_ref, outw_ref, mixed_ref,
-    flat, emb, gates, vals, quer, keys, att,
+    maps_hbm, own_hbm, pair_hbm, far_hbm, proj_hbm, outw_hbm, mixed_hbm,
+    maps_ref, own_ref, pair_ref, far_ref, proj_ref, outw_ref,
+    flat, emb, gates, vals, quer, keys, att, mixed_ref, in_sem, out_sem,
 ):
-    seq = pl.program_id(0)
-    seq_len, width = mixed_ref.shape[1:]
+    seq_dev, seq_len, width = mixed_hbm.shape
+    loads = [
+        pltpu.make_async_copy(source, target, in_sem.at[i])
+        for i, (source, target) in enumerate(
+            (
+                (maps_hbm, maps_ref), (own_hbm, own_ref), (pair_hbm, pair_ref),
+                (far_hbm, far_ref), (proj_hbm, proj_ref), (outw_hbm, outw_ref),
+            )
+        )
+    ]
+    for load in loads:
+        load.start()
+    for load in loads:
+        load.wait()
+
+    def history(seq, carry):
+        layer_history(
+            seq, maps_ref, own_ref, pair_ref, far_ref, proj_ref, outw_ref, mixed_hbm,
+            flat, emb, gates, vals, quer, keys, att, mixed_ref, out_sem,
+        )
+        return carry
+
+    lax.fori_loop(0, seq_dev, history, 0)
+    for seq in range(seq_dev):
+        for b in range(seq_len // BLOCK):
+            store_block(seq, b, mixed_ref, mixed_hbm, out_sem).wait()
+
+
+def store_block(seq, b, mixed_ref, mixed_hbm, out_sem):
+    span = pl.ds(b * BLOCK, BLOCK)
+    return pltpu.make_async_copy(
+        mixed_ref.at[seq, span], mixed_hbm.at[seq, span], out_sem.at[seq, b]
+    )
+
+
+def layer_history(
+    seq, maps_ref, own_ref, pair_ref, far_ref, proj_ref, outw_ref, mixed_hbm,
+    flat, emb, gates, vals, quer, keys, att, mixed_ref, out_sem,
+):
+    seq_len, width = mixed_hbm.shape[1:]
     head = width // HEADS
     length = maps_ref[0, seq, CAP + 16]
     rep = lax.axis_index("rep")
@@ -376,7 +451,7 @@
                         jnp.where(swapped, other, part),
                         jnp.where(swapped, part, other),
                     )
-                pair = pair_ref[span].reshape(rows, 2 * side).astype(F32)
+                pair = pair_ref[span, pl.ds(seq * cap, cap), :].reshape(rows, 2 * side).astype(F32)
                 turned = pltpu.roll(pair, side, 1)
                 parts["left"] = (pair, turned)
                 parts["right"] = (turned, pair)
@@ -457,11 +532,13 @@
                 gated, outw_ref[...], preferred_element_type=F32
             )
             live = place + b * BLOCK < length
-            mixed_ref[0, b * BLOCK : reach, :] = jnp.where(live, mixed, 0.0).astype(BF16)
+            mixed_ref[seq, b * BLOCK : reach, :] = jnp.where(live, mixed, 0.0).astype(BF16)
 
         @pl.when(b * BLOCK >= length)
         def _(b=b):
-            mixed_ref[0, b * BLOCK : (b + 1) * BLOCK, :] = jnp.zeros((BLOCK, width), BF16)
+            mixed_ref[seq, b * BLOCK : (b + 1) * BLOCK, :] = jnp.zeros((BLOCK, width), BF16)
+
+        store_block(seq, b, mixed_ref, mixed_hbm, out_sem).start()
 
 
 def layer(maps, own, pair, far, proj_weight, out_weight, seq_len):
@@ -471,18 +548,16 @@
     head = width // HEADS
     return pl.pallas_call(
         layer_kernel,
-        grid=(seq_dev,),
         out_shape=jax.ShapeDtypeStruct((seq_dev, seq_len, width), BF16),
-        in_specs=[
-            pl.BlockSpec(memory_space=pltpu.SMEM),
-            pl.BlockSpec((shards, cap, wide), lambda i: (0, 0, 0)),
-            pl.BlockSpec((shards, cap, wide), lambda i: (0, i, 0)),
-            pl.BlockSpec((shards, cap, wide), lambda i: (0, 0, 0)),
-            pl.BlockSpec((width, 4 * width), lambda i: (0, 0)),
-            pl.BlockSpec((width, width), lambda i: (0, 0)),
-        ],
-        out_specs=pl.BlockSpec((1, seq_len, width), lambda i: (i, 0, 0)),
+        in_specs=[pl.BlockSpec(memory_space=pltpu.HBM)] * 6,
+        out_specs=pl.BlockSpec(memory_space=pltpu.HBM),
         scratch_shapes=[
+            pltpu.SMEM(maps.shape, I32),
+            pltpu.VMEM(own.shape, BF16),
+            pltpu.VMEM(pair.shape, BF16),
+            pltpu.VMEM(far.shape, BF16),
+            pltpu.VMEM(proj_weight.shape, BF16),
+            pltpu.VMEM(out_weight.shape, BF16),
             pltpu.VMEM((2, shards * cap, wide), F32),
             pltpu.VMEM((2, seq_len // 16, 16, wide), F32),
             pltpu.VMEM((seq_len, width), BF16),
@@ -490,8 +565,11 @@
             pltpu.VMEM((HEADS, seq_len, head), BF16),
             pltpu.VMEM((HEADS, seq_len, head), BF16),
             pltpu.VMEM((HEADS, BLOCK, head), F32),
+            pltpu.VMEM((seq_dev, seq_len, width), BF16),
+            pltpu.SemaphoreType.DMA((6,)),
+            pltpu.SemaphoreType.DMA((seq_dev, seq_len // BLOCK)),
         ],
-        compiler_params=pltpu.CompilerParams(vmem_limit_bytes=48 * 1024 * 1024),
+        compiler_params=pltpu.CompilerParams(vmem_limit_bytes=60 * 1024 * 1024),
         name="layer",
     )(maps, own, pair, far, proj_weight, out_weight)
 

time: 106 us -> 100 us (0.943)
  local copies, waits for them, and re-layouts: 5.53 us -> 0 us
  Pallas kernels: 101 us -> 99.6 us
    unnamed x14 -> x0, local copies, waits for them, and re-layouts: 4.83 us -> none
where the time goes in v4:
time: 100 us; the launch traced here: 99.6 us
  Pallas kernels  99.6 us (100%)
    pallas_call x1, Pallas kernels, exchange_rows(): pl.pallas_call(exchange_kernel, out_shape=[jax.ShapeDtypeStruct(*shape) f...  79.9 us
    pallas_call x1, Pallas kernels, layer(): pl.pallas_call(layer_kernel, out_shape=jax.ShapeDtypeStruct((seq_dev, seq...  19.7 us

profile of v4, /device:TPU:1, one launch (start us, length us, event | category | flops | bytes accessed | tf_op | source)
XLA Modules:
  0.0 99.6 jit_solution(14735752816759931849)
XLA Ops:
  0.0 79.9 %exchange.1 = (bf16[64,32,128]{2,1,0:T(8,128)(2,1)}, bf16[64,64,128]{2,1,0:T(8,128)(2,1)}, bf16[64,32,128]{2,1,0:T(8,128)(2,1)}, s32[64,2,128]{2,1,0:T(2,128)}) custom-call(s32[2,1024]{1,0:T(2,128)} %ids_hbm.1, s32[1,128]{1,0:T(1,128)} %len_hbm.1, s32[1,128]{1,0:T(1,128)} %owner_hbm.1, s32[4096,128]{1,0:T(8,128)} %bitcast.2, bf16[64,8192]{1,0:T(8,128)(2,1)} %bitcast.3), custom_call_target="tpu_custom_call" | custom-call | tf_op jit(solution)/shard_map/exchange/pallas_call | solution.py:333
  79.9 19.7 %layer.1 = bf16[2,1024,256]{2,1,0:T(8,128)(2,1)} custom-call(s32[64,2,128]{2,1,0:T(2,128)} %get-tuple-element.9.maps_hbm, bf16[64,32,128]{2,1,0:T(8,128)(2,1)} %get-tuple-element.10.own_hbm, bf16[64,64,128]{2,1,0:T(8,128)(2,1)} %get-tuple-element.11.pair_hbm, bf16[64,32,128]{2,1,0:T(8,128)(2,1)} %get-tuple-element.12.far_hbm, bf16[256,1024]{1,0:T(8,128)(2,1)} %proj_hbm.1, ...), custom_call_target="tpu_custom_call" | custom-call | tf_op jit(solution)/shard_map/layer/pallas_call | solution.py:549

commit v5 on v4

--- a/solution.py
+++ b/solution.py
@@ -30,14 +30,17 @@
     return lax.dot_general(left, right, (((0,), (0,)), ((), ())), preferred_element_type=F32)
 
 
-def plan_order(owner_ref):
+def plan_order(owner_ref, len_ref):
     size = owner_ref.shape[1]
     row = owner_ref[...]
     col = column_of(row, size)
+    row_len = len_ref[...].astype(F32)
+    col_len = column_of(len_ref[...], size)
     sub = lax.broadcasted_iota(I32, (size, size), 0)
     lane = lax.broadcasted_iota(I32, (size, size), 1)
     keyed = row.astype(F32)
-    before = (col < keyed) | ((col == keyed) & (sub < lane))
+    sooner = (col_len > row_len) | ((col_len == row_len) & (sub < lane))
+    before = (col < keyed) | ((col == keyed) & sooner)
     rank = jnp.sum(jnp.where(before, 1.0, 0.0), axis=0, keepdims=True)
     found = jnp.where(rank == sub.astype(F32), lane.astype(F32), 0.0)
     at = jnp.sum(found, axis=1, keepdims=True)
@@ -54,7 +57,7 @@
     lax.fori_loop(0, ids_smem.shape[0], fetch, 0)
 
 
-def plan_requests(seq, length, ids_ref, stage, shards, rows_dev):
+def plan_requests(seq, length, index, ids_ref, stage, shards, rows_dev):
     seq_len = ids_ref.shape[1]
     chunk = seq_len // shards
     shift = rows_dev.bit_length() - 1
@@ -99,16 +102,18 @@
     lanes = lax.broadcasted_iota(I32, (shards, 128), 1)
     result = result.astype(I32)
     result = jnp.where(lanes < CAP, result & (rows_dev - 1), result & (shards * CAP - 1))
-    return jnp.where(lanes == CAP + 16, length, result)
+    result = jnp.where(lanes == CAP + 16, length, result)
+    return jnp.where(lanes == CAP + 17, index, result)
 
 
 def exchange_kernel(
-    ids_hbm, len_hbm, owner_hbm, home_ref, table_ref,
-    own_got, pair_got, far_got, maps_got,
-    ids_ref, ids_lines, ids_smem, len_smem, owner_ref, home_in, lines, asked_ref, asked_all, asked_smem, order_in, order_ref, table_in, left_in, right_in, far_in,
+    ids_hbm, len_hbm, owner_hbm, home_ref, table_ref, proj_hbm, outw_hbm,
+    own_hbm, late_got, far_hbm, maps_hbm, first_hbm,
+    ids_ref, ids_lines, ids_smem, len_smem, len_ref, owner_ref, home_in, lines, asked_ref, asked_all, asked_smem, order_in, order_ref, table_in, left_in, right_in, far_in,
     own_rows, pair_rows, far_rows, stage,
-    own_out, pair_out, far_out, maps_out,
-    local_sem, asked_send, asked_recv, side_send, side_recv, row_send, row_recv,
+    own_out, pair_out, far_out, maps_out, late_out,
+    own_got, pair_got, far_got, maps_got, maps_smem, proj_ref, outw_ref,
+    flat, emb, gates, vals, quer, keys, att, mixed_ref, out_sem, local_sem, asked_send, asked_recv, side_send, side_recv, row_send, row_recv,
 ):
     shards = own_got.shape[0]
     reps = 4
@@ -125,6 +130,10 @@
     load_ids = pltpu.make_async_copy(ids_hbm, ids_ref, local_sem.at[2])
     load_owner = pltpu.make_async_copy(owner_hbm, owner_ref, local_sem.at[3])
     load_len = pltpu.make_async_copy(len_hbm, len_smem, local_sem.at[4])
+    load_lens = pltpu.make_async_copy(len_hbm, len_ref, local_sem.at[13])
+    load_proj = pltpu.make_async_copy(proj_hbm, proj_ref, local_sem.at[14])
+    load_outw = pltpu.make_async_copy(outw_hbm, outw_ref, local_sem.at[15])
+    load_lens.start()
     load_ids.start()
     load_owner.start()
     load_len.start()
@@ -181,7 +190,10 @@
             at = seq * (seq_len // 128) + b
             ids_lines[at : at + 1, :] = ids_ref[seq : seq + 1, b * 128 : (b + 1) * 128]
     load_owner.wait()
-    order_in[...] = plan_order(owner_ref)
+    load_lens.wait()
+    load_proj.start()
+    load_outw.start()
+    order_in[...] = plan_order(owner_ref, len_ref)
     spill_ids = pltpu.make_async_copy(ids_lines, ids_smem, local_sem.at[5])
     spill_ids.start()
     spill_ids.wait()
@@ -216,8 +228,11 @@
     to_right.start()
     to_left.start()
     for seq in range(seq_dev):
-        length = len_smem[0, me * seq_dev + seq]
-        asked_ref[:, seq, :] = plan_requests(seq, length, ids_ref, lines, shards, rows_dev)
+        index = me * seq_dev + seq
+        length = len_smem[0, index]
+        asked_ref[:, seq, :] = plan_requests(
+            seq, length, index, ids_ref, lines, shards, rows_dev
+        )
 
     def ask(i, carry):
         peer = peer_at(i)
@@ -250,7 +265,7 @@
         local.start()
         return local
 
-    def sweep(pick, out, got, kind, paired, extra=None):
+    def sweep(pick, out, got, kind, of, extra=None):
         def owner(i, carry):
             peer = peer_at(i)
             hists = [order_ref[0, 2 * peer + q] for q in range(2)]
@@ -262,19 +277,19 @@
             sources = [lax.shift_right_logical(hist, 1) for hist in hists]
             halves = [hist & 1 for hist in hists]
             slot = lax.rem(i, 2)
-            if paired:
+            if len(of) == 2:
                 for j in range(CAP):
                     one = pick[pl.ds(asked_smem[sources[0], halves[0], j], 1), :]
                     two = pick[pl.ds(asked_smem[sources[1], halves[1], j], 1), :]
                     stage[slot, pl.ds(j, 1), :] = jnp.where(first_half, one, two)
                 out[peer] = stage[slot, :CAP, :].astype(BF16)
             else:
-                for q in range(2):
-                    for j in range(CAP):
-                        stage[slot, pl.ds(q * CAP + j, 1), :] = pick[
-                            pl.ds(asked_smem[sources[q], halves[q], j], 1), :
-                        ]
-                out[peer] = stage[slot].astype(BF16)
+                q = of[0]
+                for j in range(CAP):
+                    stage[slot, pl.ds(j, 1), :] = pick[
+                        pl.ds(asked_smem[sources[q], halves[q], j], 1), :
+                    ]
+                out[peer] = stage[slot, :CAP, :].astype(BF16)
 
             @pl.when(i > 0)
             def _():
@@ -287,7 +302,7 @@
 
         lax.fori_loop(0, shards, owner, 0)
 
-    sweep(own_rows, own_out, own_got, 0, True, maps_out)
+    sweep(own_rows, own_out, own_got, 0, (0, 1), maps_out)
     to_right.wait_recv()
     to_left.wait_recv()
     half = cols // 2
@@ -297,49 +312,105 @@
     on_left.start()
     turn(left_in, right_in, pair_rows)
     stays = [stay(own_out, own_got, 0), stay(maps_out, maps_got, 3)]
-    sweep(pair_rows, pair_out, pair_got, 1, False)
+    sweep(pair_rows, pair_out, pair_got, 1, (0,))
     on_right.wait_recv()
     on_left.wait_recv()
     turn(far_in, far_in, far_rows)
     stays.append(stay(pair_out, pair_got, 1))
-    sweep(far_rows, far_out, far_got, 2, True)
+    sweep(far_rows, far_out, far_got, 2, (0, 1))
+    sweep(pair_rows, late_out, late_got, 4, (1,))
+    stays.append(stay(far_out, far_got, 2))
+    for local in stays:
+        local.wait()
+    late_stay = stay(late_out, late_got, 7)
+    pairs = {
+        0: (own_out, own_got),
+        1: (pair_out, pair_got),
+        2: (far_out, far_got),
+        3: (maps_out, maps_got),
+        4: (late_out, late_got),
+    }
+
+    def shared(kind):
+        out, got = pairs[kind]
+        return shard_copy(
+            out.at[others], got.at[others], row_send.at[kind], row_recv.at[kind], me
+        )
+
+    for kind in (3, 0, 1, 2):
+        shared(kind).wait_recv()
+    kept = [
+        pltpu.make_async_copy(source, target, local_sem.at[17 + i])
+        for i, (source, target) in enumerate(
+            ((maps_got, maps_smem), (maps_got, maps_hbm), (own_got, own_hbm), (far_got, far_hbm))
+        )
+    ]
+    for copy in kept:
+        copy.start()
+    kept[0].wait()
+    load_proj.wait()
+    load_outw.wait()
+
+    def put(b):
+        return store_block(b, mixed_ref, first_hbm, out_sem)
+
+    layer_history(
+        0, True, maps_smem, own_got, pair_got, far_got, proj_ref, outw_ref, put,
+        flat, emb, gates, vals, quer, keys, att, mixed_ref,
+    )
+    for b in range(seq_len // BLOCK):
+        put(b).wait()
+    for copy in kept[1:]:
+        copy.wait()
+    late_stay.wait()
+    shared(4).wait_recv()
     for copy in (to_right, to_left, on_right, on_left):
         copy.wait_send()
-    stays.append(stay(far_out, far_got, 2))
-    for kind, (out, got) in enumerate(
-        ((own_out, own_got), (pair_out, pair_got), (far_out, far_got), (maps_out, maps_got))
-    ):
-        shard_copy(
-            out.at[others], got.at[others], row_send.at[kind], row_recv.at[kind], me
-        ).wait()
-    for local in stays:
-        local.wait()
-
-
-def exchange_rows(item_ids, lengths, owners, row_home, table, shards):
+    for kind in range(5):
+        shared(kind).wait_send()
+
+
+def layer_scratch(seq_len, width, slots):
+    head = width // HEADS
+    wide = width // 2
+    return [
+        pltpu.VMEM((2, slots, wide), F32),
+        pltpu.VMEM((2, seq_len // 16, 16, wide), F32),
+        pltpu.VMEM((seq_len, width), BF16),
+        pltpu.VMEM((HEADS, seq_len, head), BF16),
+        pltpu.VMEM((HEADS, seq_len, head), BF16),
+        pltpu.VMEM((HEADS, seq_len, head), BF16),
+        pltpu.VMEM((HEADS, BLOCK, head), F32),
+        pltpu.VMEM((seq_len, width), BF16),
+        pltpu.SemaphoreType.DMA((seq_len // BLOCK,)),
+    ]
+
+
+def exchange_rows(
+    item_ids, lengths, owners, row_home, table, proj_weight, out_weight, shards
+):
     cols, rows_dev = table.shape
     seq_dev, seq_len = item_ids.shape
     wide = 2 * cols
     any_space = pl.BlockSpec(memory_space=pl.ANY)
     hbm_space = pl.BlockSpec(memory_space=pltpu.HBM)
     lines = seq_dev * seq_len // 128
-    shapes = (
-        ((shards, CAP, wide), BF16),
-        ((shards, 2 * CAP, wide), BF16),
-        ((shards, CAP, wide), BF16),
-        ((shards, seq_dev, 128), I32),
-    )
+    block = ((shards, CAP, wide), BF16)
+    maps = ((shards, seq_dev, 128), I32)
+    width = proj_weight.shape[0]
+    outs = (block, block, block, maps, ((seq_len, width), BF16))
     home = row_home.reshape(-1, 128)
     return pl.pallas_call(
         exchange_kernel,
-        out_shape=[jax.ShapeDtypeStruct(*shape) for shape in shapes],
-        in_specs=[hbm_space] * 5,
-        out_specs=[any_space] * 4,
+        out_shape=[jax.ShapeDtypeStruct(*shape) for shape in outs],
+        in_specs=[hbm_space] * 7,
+        out_specs=[any_space] * 5,
         scratch_shapes=[
             pltpu.VMEM(item_ids.shape, I32),
             pltpu.VMEM((lines, 128), I32),
             pltpu.SMEM((lines, 128), I32),
             pltpu.SMEM(lengths.shape, I32),
+            pltpu.VMEM(lengths.shape, I32),
             pltpu.VMEM(owners.shape, I32),
             pltpu.VMEM(home.shape, I32),
             pltpu.VMEM((lines, 128, 128), I32),
@@ -355,21 +426,26 @@
             pltpu.VMEM((rows_dev, wide), F32),
             pltpu.VMEM((rows_dev, wide), F32),
             pltpu.VMEM((rows_dev, wide), F32),
-            pltpu.VMEM((2, 2 * CAP, wide), F32),
-            *[pltpu.VMEM(*shape) for shape in shapes],
-            pltpu.SemaphoreType.DMA((13,)),
+            pltpu.VMEM((2, CAP, wide), F32),
+            *[pltpu.VMEM(*shape) for shape in (block, block, block, maps, block)],
+            *[pltpu.VMEM(*shape) for shape in (block, block, block, maps)],
+            pltpu.SMEM(*maps),
+            pltpu.VMEM(proj_weight.shape, BF16),
+            pltpu.VMEM(out_weight.shape, BF16),
+            *layer_scratch(seq_len, width, shards * CAP),
+            pltpu.SemaphoreType.DMA((21,)),
             pltpu.SemaphoreType.DMA,
             pltpu.SemaphoreType.DMA,
             pltpu.SemaphoreType.DMA((4,)),
             pltpu.SemaphoreType.DMA((4,)),
-            pltpu.SemaphoreType.DMA((4,)),
-            pltpu.SemaphoreType.DMA((4,)),
+            pltpu.SemaphoreType.DMA((5,)),
+            pltpu.SemaphoreType.DMA((5,)),
         ],
         compiler_params=pltpu.CompilerParams(
             collective_id=0, has_side_effects=True, vmem_limit_bytes=60 * 1024 * 1024
         ),
         name="exchange",
-    )(item_ids, lengths, owners, home, table)
+    )(item_ids, lengths, owners, home, table, proj_weight, out_weight)
 
 
 def normed_rows(values):
@@ -383,17 +459,18 @@
 
 
 def layer_kernel(
-    maps_hbm, own_hbm, pair_hbm, far_hbm, proj_hbm, outw_hbm, mixed_hbm,
-    maps_ref, own_ref, pair_ref, far_ref, proj_ref, outw_ref,
-    flat, emb, gates, vals, quer, keys, att, mixed_ref, in_sem, out_sem,
+    maps_hbm, own_hbm, late_hbm, far_hbm, proj_hbm, outw_hbm, first_hbm, mixed_hbm,
+    maps_ref, own_ref, late_ref, far_ref, proj_ref, outw_ref, first_ref,
+    flat, emb, gates, vals, quer, keys, att, mixed_ref, out_sem, in_sem,
 ):
-    seq_dev, seq_len, width = mixed_hbm.shape
+    seq_len = mixed_hbm.shape[1]
     loads = [
         pltpu.make_async_copy(source, target, in_sem.at[i])
         for i, (source, target) in enumerate(
             (
-                (maps_hbm, maps_ref), (own_hbm, own_ref), (pair_hbm, pair_ref),
+                (maps_hbm, maps_ref), (own_hbm, own_ref), (late_hbm, late_ref),
                 (far_hbm, far_ref), (proj_hbm, proj_ref), (outw_hbm, outw_ref),
+                (first_hbm, first_ref),
             )
         )
     ]
@@ -401,32 +478,31 @@
         load.start()
     for load in loads:
         load.wait()
-
-    def history(seq, carry):
-        layer_history(
-            seq, maps_ref, own_ref, pair_ref, far_ref, proj_ref, outw_ref, mixed_hbm,
-            flat, emb, gates, vals, quer, keys, att, mixed_ref, out_sem,
-        )
-        return carry
-
-    lax.fori_loop(0, seq_dev, history, 0)
-    for seq in range(seq_dev):
-        for b in range(seq_len // BLOCK):
-            store_block(seq, b, mixed_ref, mixed_hbm, out_sem).wait()
-
-
-def store_block(seq, b, mixed_ref, mixed_hbm, out_sem):
+    long_at = jnp.where(maps_ref[0, 0, CAP + 17] > maps_ref[0, 1, CAP + 17], 1, 0)
+    move = pltpu.make_async_copy(first_ref, mixed_hbm.at[long_at], in_sem.at[7])
+    move.start()
+
+    def put(b):
+        return store_block(b, mixed_ref, mixed_hbm.at[1 - long_at], out_sem)
+
+    layer_history(
+        1, False, maps_ref, own_ref, late_ref, far_ref, proj_ref, outw_ref, put,
+        flat, emb, gates, vals, quer, keys, att, mixed_ref, move.wait,
+    )
+    for b in range(seq_len // BLOCK):
+        put(b).wait()
+
+
+def store_block(b, mixed_ref, mixed_hbm, out_sem):
     span = pl.ds(b * BLOCK, BLOCK)
-    return pltpu.make_async_copy(
-        mixed_ref.at[seq, span], mixed_hbm.at[seq, span], out_sem.at[seq, b]
-    )
+    return pltpu.make_async_copy(mixed_ref.at[span], mixed_hbm.at[span], out_sem.at[b])
 
 
 def layer_history(
-    seq, maps_ref, own_ref, pair_ref, far_ref, proj_ref, outw_ref, mixed_hbm,
-    flat, emb, gates, vals, quer, keys, att, mixed_ref, out_sem,
+    seq, whole, maps_ref, own_ref, pair_ref, far_ref, proj_ref, outw_ref, put,
+    flat, emb, gates, vals, quer, keys, att, mixed_ref, ready=None,
 ):
-    seq_len, width = mixed_hbm.shape[1:]
+    seq_len, width = mixed_ref.shape
     head = width // HEADS
     length = maps_ref[0, seq, CAP + 16]
     rep = lax.axis_index("rep")
@@ -434,8 +510,6 @@
     side = width // 4
     group = 8
     first_half = lax.broadcasted_iota(I32, (1, 2 * side), 1) < side
-    swapped = seq == 1
-
     for r in range(4):
 
         @pl.when(rep == r)
@@ -447,11 +521,8 @@
                 for name, ref in (("own", own_ref), ("far", far_ref)):
                     part = ref[span].reshape(rows, 2 * side).astype(F32)
                     other = pltpu.roll(part, side, 1)
-                    parts[name] = (
-                        jnp.where(swapped, other, part),
-                        jnp.where(swapped, part, other),
-                    )
-                pair = pair_ref[span, pl.ds(seq * cap, cap), :].reshape(rows, 2 * side).astype(F32)
+                    parts[name] = (part, other) if seq == 0 else (other, part)
+                pair = pair_ref[span].reshape(rows, 2 * side).astype(F32)
                 turned = pltpu.roll(pair, side, 1)
                 parts["left"] = (pair, turned)
                 parts["right"] = (turned, pair)
@@ -474,13 +545,13 @@
                 emb[tile, c, pl.ds(i, 1), :] = flat[tile, pl.ds(slot, 1), :]
         return carry
 
-    lax.fori_loop(0, (length + unroll - 1) // unroll, fetch, 0)
+    lax.fori_loop(0, seq_len // unroll if whole else (length + unroll - 1) // unroll, fetch, 0)
 
     def rows_of(b):
         span = pl.ds(b * (BLOCK // unroll), BLOCK // unroll)
         return jnp.concatenate([emb[t, span].reshape(BLOCK, 2 * side) for t in range(2)], axis=1)
 
-    blocks = (length + BLOCK - 1) // BLOCK
+    blocks = seq_len // BLOCK if whole else (length + BLOCK - 1) // BLOCK
     place = lax.broadcasted_iota(I32, (BLOCK, 1), 0)
 
     def project(b, carry):
@@ -504,83 +575,77 @@
 
     lax.fori_loop(0, blocks, project, 0)
     inverse = 1.0 / length.astype(F32)
+    if ready is not None:
+        ready()
+    keep = lax.broadcasted_iota(I32, (BLOCK, BLOCK), 1) <= lax.broadcasted_iota(
+        I32, (BLOCK, BLOCK), 0
+    )
+
+    def run(b):
+        reach = (b + 1) * BLOCK
+
+        def attend(h, carry):
+            query = quer[h, b * BLOCK : reach, :]
+            scores = lax.dot_general(
+                query, keys[h, :reach, :], (((1,), (1,)), ((), ())), preferred_element_type=F32
+            )
+            weights = gated_linear(scores)
+            last = jnp.where(keep, weights[:, b * BLOCK :], 0.0).astype(BF16)
+            if b:
+                last = jnp.concatenate([weights[:, : b * BLOCK].astype(BF16), last], axis=1)
+            att[h] = jnp.dot(last, vals[h, :reach, :], preferred_element_type=F32)
+            return carry
+
+        lax.fori_loop(0, HEADS, attend, 0)
+        joined = jnp.concatenate([att[h] for h in range(HEADS)], axis=1) * inverse
+        gated = (normed_rows(joined) * gates[b * BLOCK : reach, :].astype(F32)).astype(BF16)
+        mixed = rows_of(b) + jnp.dot(gated, outw_ref[...], preferred_element_type=F32)
+        live = place + b * BLOCK < length
+        mixed_ref[b * BLOCK : reach, :] = jnp.where(live, mixed, 0.0).astype(BF16)
+
     for b in range(seq_len // BLOCK):
-
-        @pl.when(b * BLOCK < length)
-        def _(b=b):
-            reach = (b + 1) * BLOCK
-            keep = lax.broadcasted_iota(I32, (BLOCK, BLOCK), 1) <= lax.broadcasted_iota(
-                I32, (BLOCK, BLOCK), 0
-            )
-
-            def attend(h, carry):
-                query = quer[h, b * BLOCK : reach, :]
-                scores = lax.dot_general(
-                    query, keys[h, :reach, :], (((1,), (1,)), ((), ())), preferred_element_type=F32
-                )
-                weights = gated_linear(scores)
-                last = jnp.where(keep, weights[:, b * BLOCK :], 0.0).astype(BF16)
-                if b:
-                    last = jnp.concatenate([weights[:, : b * BLOCK].astype(BF16), last], axis=1)
-                att[h] = jnp.dot(last, vals[h, :reach, :], preferred_element_type=F32)
-                return carry
-
-            lax.fori_loop(0, HEADS, attend, 0)
-            whole = jnp.concatenate([att[h] for h in range(HEADS)], axis=1) * inverse
-            gated = (normed_rows(whole) * gates[b * BLOCK : reach, :].astype(F32)).astype(BF16)
-            mixed = rows_of(b) + jnp.dot(
-                gated, outw_ref[...], preferred_element_type=F32
-            )
-            live = place + b * BLOCK < length
-            mixed_ref[seq, b * BLOCK : reach, :] = jnp.where(live, mixed, 0.0).astype(BF16)
-
-        @pl.when(b * BLOCK >= length)
-        def _(b=b):
-            mixed_ref[seq, b * BLOCK : (b + 1) * BLOCK, :] = jnp.zeros((BLOCK, width), BF16)
-
-        store_block(seq, b, mixed_ref, mixed_hbm, out_sem).start()
-
-
-def layer(maps, own, pair, far, proj_weight, out_weight, seq_len):
-    shards, cap, wide = own.shape
-    seq_dev = 2
-    width = proj_weight.shape[0]
-    head = width // HEADS
+        if whole:
+            run(b)
+        else:
+            pl.when(b * BLOCK < length)(lambda b=b: run(b))
+
+            @pl.when(b * BLOCK >= length)
+            def _(b=b):
+                mixed_ref[b * BLOCK : (b + 1) * BLOCK, :] = jnp.zeros((BLOCK, width), BF16)
+
+        put(b).start()
+
+
+def layer(maps, own, late, far, first, proj_weight, out_weight):
+    slots = own.shape[0] * own.shape[1]
+    seq_len, width = first.shape
     return pl.pallas_call(
         layer_kernel,
-        out_shape=jax.ShapeDtypeStruct((seq_dev, seq_len, width), BF16),
-        in_specs=[pl.BlockSpec(memory_space=pltpu.HBM)] * 6,
+        out_shape=jax.ShapeDtypeStruct((maps.shape[1], seq_len, width), BF16),
+        in_specs=[pl.BlockSpec(memory_space=pltpu.HBM)] * 7,
         out_specs=pl.BlockSpec(memory_space=pltpu.HBM),
         scratch_shapes=[
             pltpu.SMEM(maps.shape, I32),
             pltpu.VMEM(own.shape, BF16),
-            pltpu.VMEM(pair.shape, BF16),
+            pltpu.VMEM(late.shape, BF16),
             pltpu.VMEM(far.shape, BF16),
             pltpu.VMEM(proj_weight.shape, BF16),
             pltpu.VMEM(out_weight.shape, BF16),
-            pltpu.VMEM((2, shards * cap, wide), F32),
-            pltpu.VMEM((2, seq_len // 16, 16, wide), F32),
-            pltpu.VMEM((seq_len, width), BF16),
-            pltpu.VMEM((HEADS, seq_len, head), BF16),
-            pltpu.VMEM((HEADS, seq_len, head), BF16),
-            pltpu.VMEM((HEADS, seq_len, head), BF16),
-            pltpu.VMEM((HEADS, BLOCK, head), F32),
-            pltpu.VMEM((seq_dev, seq_len, width), BF16),
-            pltpu.SemaphoreType.DMA((6,)),
-            pltpu.SemaphoreType.DMA((seq_dev, seq_len // BLOCK)),
+            pltpu.VMEM(first.shape, BF16),
+            *layer_scratch(seq_len, width, slots),
+            pltpu.SemaphoreType.DMA((8,)),
         ],
         compiler_params=pltpu.CompilerParams(vmem_limit_bytes=60 * 1024 * 1024),
         name="layer",
-    )(maps, own, pair, far, proj_weight, out_weight)
+    )(maps, own, late, far, proj_weight, out_weight, first)
 
 
 def body(item_ids, seq_lengths, seq_owner, row_home, item_table, proj_weight, out_weight):
     shards = lax.axis_size("shard")
-    seq_len = item_ids.shape[1]
-    own, pair, far, maps = exchange_rows(
-        item_ids, seq_lengths, seq_owner, row_home, item_table.T, shards
+    own, late, far, maps, first = exchange_rows(
+        item_ids, seq_lengths, seq_owner, row_home, item_table.T, proj_weight, out_weight, shards
     )
-    return layer(maps, own, pair, far, proj_weight, out_weight, seq_len)
+    return layer(maps, own, late, far, first, proj_weight, out_weight)
 
 
 def solution(mesh):

time: 100 us -> 96.2 us (0.962)
  Pallas kernels: 99.6 us -> 95.1 us
    pallas_call x1, Pallas kernels: 19.7 us -> 6.35 us  [layer(): pl.pallas_call(layer_kernel, out_shape=jax.ShapeDtypeStruct((maps.shape[1...]
    pallas_call x1, Pallas kernels: 79.9 us -> 88.7 us  [exchange_rows(): pl.pallas_call(exchange_kernel, out_shape=[jax.ShapeDtypeStruct(*shape) f...]
where the time goes in v5:
time: 96.2 us; the launch traced here: 95.1 us
  Pallas kernels  95.1 us (99%)
    pallas_call x1, Pallas kernels, exchange_rows(): pl.pallas_call(exchange_kernel, out_shape=[jax.ShapeDtypeStruct(*shape) f...  88.7 us
    pallas_call x1, Pallas kernels, layer(): pl.pallas_call(layer_kernel, out_shape=jax.ShapeDtypeStruct((maps.shape[1...  6.35 us

profile of v5, /device:TPU:1, one launch (start us, length us, event | category | flops | bytes accessed | tf_op | source)
XLA Modules:
  0.0 95.1 jit_solution(1256052630525471210)
XLA Ops:
  0.0 88.7 %exchange.1 = (bf16[64,32,128]{2,1,0:T(8,128)(2,1)}, bf16[64,32,128]{2,1,0:T(8,128)(2,1)}, bf16[64,32,128]{2,1,0:T(8,128)(2,1)}, s32[64,2,128]{2,1,0:T(2,128)}, bf16[1024,256]{1,0:T(8,128)(2,1)}) custom-call(s32[2,1024]{1,0:T(2,128)} %ids_hbm.1, s32[1,128]{1,0:T(1,128)} %len_hbm.1, s32[1,128]{1,0:T(1,128)} %owner_hbm.1, s32[4096,128]{1,0:T(8,128)} %bitcast.2, ...), custom_call_target="tpu_custom_call" | custom-call | tf_op jit(solution)/shard_map/exchange/pallas_call | solution.py:403
  88.8 6.4 %layer.1 = bf16[2,1024,256]{2,1,0:T(8,128)(2,1)} custom-call(s32[64,2,128]{2,1,0:T(2,128)} %get-tuple-element.10.maps_hbm, bf16[64,32,128]{2,1,0:T(8,128)(2,1)} %get-tuple-element.11.own_hbm, bf16[64,32,128]{2,1,0:T(8,128)(2,1)} %get-tuple-element.12.late_hbm, bf16[64,32,128]{2,1,0:T(8,128)(2,1)} %get-tuple-element.13.far_hbm, bf16[256,1024]{1,0:T(8,128)(2,1)} %proj_hbm.3, ...), custom_call_target="tpu_custom_call" | custom-call | tf_op jit(solution)/shard_map/layer/pallas_call | solution.py:622

commit v6 on v5

v6 whole, which is shorter than its diff:
```python
import math

import jax
import jax.numpy as jnp
from jax import lax
from jax.experimental import pallas as pl
from jax.experimental.pallas import tpu as pltpu
from jax.sharding import PartitionSpec as P

HEADS = 4
EPSILON = 1e-06
BLOCK = 256
CAP = 32
F32 = jnp.float32
BF16 = jnp.bfloat16
I32 = jnp.int32


def column_of(row, size):
    pieces = []
    step = 128
    eye = lax.broadcasted_iota(I32, (step, step), 0) == lax.broadcasted_iota(I32, (step, step), 1)
    for i in range(size // step):
        part = row[:, i * step : (i + 1) * step].astype(F32)
        pieces.append(jnp.sum(jnp.where(eye, part, 0.0), axis=1, keepdims=True))
    return jnp.concatenate(pieces, axis=0)


def contract_rows(left, right):
    return lax.dot_general(left, right, (((0,), (0,)), ((), ())), preferred_element_type=F32)


def plan_order(owner_ref, len_ref):
    size = owner_ref.shape[1]
    row = owner_ref[...]
    col = column_of(row, size)
    row_len = len_ref[...].astype(F32)
    col_len = column_of(len_ref[...], size)
    sub = lax.broadcasted_iota(I32, (size, size), 0)
    lane = lax.broadcasted_iota(I32, (size, size), 1)
    keyed = row.astype(F32)
    sooner = (col_len > row_len) | ((col_len == row_len) & (sub < lane))
    before = (col < keyed) | ((col == keyed) & sooner)
    rank = jnp.sum(jnp.where(before, 1.0, 0.0), axis=0, keepdims=True)
    found = jnp.where(rank == sub.astype(F32), lane.astype(F32), 0.0)
    at = jnp.sum(found, axis=1, keepdims=True)
    return jnp.sum(jnp.where(sub == lane, at, 0.0), axis=0, keepdims=True).astype(I32) & (size - 1)


def plan_fetch(ids_smem, home, stage):
    def fetch(c, carry):
        for i in range(128):
            line = lax.shift_right_logical(ids_smem[c, i], 7)
            stage[c, pl.ds(i, 1), :] = home[pl.ds(line, 1), :]
        return carry

    lax.fori_loop(0, ids_smem.shape[0], fetch, 0)


def plan_requests(seq, length, index, ids_ref, stage, shards, rows_dev):
    seq_len = ids_ref.shape[1]
    chunk = seq_len // shards
    shift = rows_dev.bit_length() - 1
    place = lax.broadcasted_iota(I32, (128, 1), 0)
    lane = lax.broadcasted_iota(I32, (128, 128), 1)
    lane_k = lax.broadcasted_iota(I32, (128, shards), 1)
    sub = lax.broadcasted_iota(I32, (128, 128), 0)
    below = (lane < sub).astype(BF16)
    eye = lane == sub
    carry = jnp.zeros((1, shards), F32)
    lefts, rights = [], []
    owns, slots = [], []
    for b in range(seq_len // 128):
        ids = jnp.sum(
            jnp.where(eye, (ids_ref[seq : seq + 1, b * 128 : (b + 1) * 128] & 127).astype(F32), 0.0),
            axis=1,
            keepdims=True,
        )
        lines = stage[seq * (seq_len // 128) + b].astype(F32)
        home = jnp.sum(
            jnp.where(ids == lane.astype(F32), lines, 0.0), axis=1, keepdims=True
        ).astype(I32)
        at = place + b * 128
        target = jnp.where(at < length, lax.shift_right_logical(home, shift), shards)
        row = home & (rows_dev - 1)
        onehot = jnp.where(target == lane_k, 1.0, 0.0)
        onehot16 = onehot.astype(BF16)
        before = jnp.dot(below, onehot16, preferred_element_type=F32) + carry
        rank = jnp.sum(before * onehot, axis=1, keepdims=True)
        carry = carry + jnp.sum(onehot, axis=0, keepdims=True)
        at_rank = lane.astype(F32) == rank
        lefts += [onehot16, onehot16]
        rights.append(jnp.where(at_rank, (row & ~127).astype(F32), 0.0).astype(BF16))
        rights.append(jnp.where(at_rank, (row & 127).astype(F32), 0.0).astype(BF16))
        slot = jnp.where(at < length, target * CAP + rank.astype(I32), 0)
        own = jnp.where(at // chunk == lane_k, 1.0, 0.0).astype(BF16)
        at_place = lane == lax.rem(at, chunk) + CAP
        lefts += [own, own]
        rights.append(jnp.where(at_place, (slot & ~127).astype(F32), 0.0).astype(BF16))
        rights.append(jnp.where(at_place, (slot & 127).astype(F32), 0.0).astype(BF16))
    result = contract_rows(jnp.concatenate(lefts, axis=0), jnp.concatenate(rights, axis=0))
    lanes = lax.broadcasted_iota(I32, (shards, 128), 1)
    result = result.astype(I32)
    result = jnp.where(lanes < CAP, result & (rows_dev - 1), result & (shards * CAP - 1))
    result = jnp.where(lanes == CAP + 16, length, result)
    return jnp.where(lanes == CAP + 17, index, result)


def exchange_kernel(
    ids_hbm, len_hbm, owner_hbm, home_ref, table_ref, proj_hbm, outw_hbm,
    late_got, maps_hbm, first_hbm,
    ids_ref, ids_lines, ids_smem, len_smem, len_ref, owner_ref, home_in, lines,
    asked_ref, asked_all, asked_smem, order_all, order_smem, table_in, rows, stage,
    soon_out, late_out, maps_out, soon_got, maps_got, maps_smem, proj_ref, outw_ref,
    flat, emb, gates, vals, quer, keys, att, mixed_ref, out_sem, local_sem,
    asked_send, asked_recv, order_send, order_recv, row_send, row_recv,
):
    shards = maps_hbm.shape[0]
    reps = asked_all.shape[0] // shards
    seq_dev, seq_len = ids_ref.shape
    cols, rows_dev = table_ref.shape
    me = lax.axis_index("shard")
    rep = lax.axis_index("rep")
    here = rep * shards + me
    chunk = min(256, rows_dev)
    half = CAP // 2

    load = pltpu.make_async_copy(table_ref, table_in, local_sem.at[0])
    load_home = pltpu.make_async_copy(home_ref, home_in, local_sem.at[1])
    load_ids = pltpu.make_async_copy(ids_hbm, ids_ref, local_sem.at[2])
    load_owner = pltpu.make_async_copy(owner_hbm, owner_ref, local_sem.at[3])
    load_len = pltpu.make_async_copy(len_hbm, len_smem, local_sem.at[4])
    load_lens = pltpu.make_async_copy(len_hbm, len_ref, local_sem.at[5])
    load_proj = pltpu.make_async_copy(proj_hbm, proj_ref, local_sem.at[6])
    load_outw = pltpu.make_async_copy(outw_hbm, outw_ref, local_sem.at[7])
    load_ids.start()
    load_owner.start()
    load_len.start()
    load_lens.start()
    load_home.start()
    load.start()
    barrier = pltpu.get_barrier_semaphore()

    depth = min(8, shards // 2)
    spread = shards // (2 * depth)

    def toward(i, size):
        step = (i + 1) // 2
        return lax.rem(size // 2 + step * (2 * lax.rem(i, 2) - 1) + size, size)

    def peer_at(i):
        dz = toward(i // (2 * spread), depth)
        dx = toward(lax.rem(i // 2, spread), spread)
        core = lax.rem(lax.rem(me, 2) + 1 + lax.rem(i, 2), 2)
        z = lax.rem(me // 2 + dz, depth)
        x = lax.rem(me // (2 * depth) + dx, spread)
        return (x * depth + z) * 2 + core

    def greet(i, carry):
        other = lax.rem(here + i, reps * shards)
        pl.semaphore_signal(
            barrier,
            inc=1,
            device_id={"rep": other // shards, "shard": lax.rem(other, shards)},
            device_id_type=pl.DeviceIdType.MESH,
        )
        return carry

    lax.fori_loop(1, reps * shards, greet, 0)

    eye = (
        lax.broadcasted_iota(I32, (chunk, chunk), 0) == lax.broadcasted_iota(I32, (chunk, chunk), 1)
    ).astype(BF16)

    def turn(c, carry):
        at = pl.multiple_of(c * chunk, chunk)
        part = table_in[:, pl.ds(at, chunk)]
        rows[pl.ds(at, chunk), :] = lax.dot_general(
            eye,
            jnp.concatenate([part, part], axis=0),
            (((1,), (1,)), ((), ())),
            preferred_element_type=F32,
        )
        return carry

    load_ids.wait()
    for seq in range(seq_dev):
        for b in range(seq_len // 128):
            at = seq * (seq_len // 128) + b
            ids_lines[at : at + 1, :] = ids_ref[seq : seq + 1, b * 128 : (b + 1) * 128]
    spill_ids = pltpu.make_async_copy(ids_lines, ids_smem, local_sem.at[8])
    spill_ids.start()
    load_owner.wait()
    load_lens.wait()
    order_all[rep] = plan_order(owner_ref, len_ref)
    spill_ids.wait()
    load_home.wait()
    plan_fetch(ids_smem, home_in, lines)
    load_len.wait()
    for seq in range(seq_dev):
        index = me * seq_dev + seq
        length = len_smem[0, index]
        asked_ref[:, seq, :] = plan_requests(
            seq, length, index, ids_ref, lines, shards, rows_dev
        )
    load.wait()
    load_proj.start()
    load_outw.start()
    pl.semaphore_wait(barrier, reps * shards - 1)

    def copy_to(source, target, send, recv, other, peer):
        return pltpu.make_async_remote_copy(
            src_ref=source,
            dst_ref=target,
            send_sem=send,
            recv_sem=recv,
            device_id={"rep": other, "shard": peer},
            device_id_type=pl.DeviceIdType.MESH,
        )

    def ask(i, carry):
        peer = peer_at(i)
        for turn_by in range(reps):
            other = lax.rem(rep + turn_by, reps)

            def go():
                copy_to(
                    asked_ref.at[peer], asked_all.at[here], asked_send, asked_recv, other, peer
                ).start()

            if turn_by == 0:
                pl.when(i < shards - 1)(go)
            else:
                go()
        return carry

    lax.fori_loop(0, shards, ask, 0)
    keep = pltpu.make_async_copy(asked_ref.at[me], asked_all.at[here], local_sem.at[9])
    keep.start()
    orders = [
        copy_to(
            order_all.at[rep],
            order_all.at[rep],
            order_send.at[i],
            order_recv.at[i],
            lax.rem(rep + 1 + i, reps),
            me,
        )
        for i in range(reps - 1)
    ]
    for copy in orders:
        copy.start()
    lax.fori_loop(0, rows_dev // chunk, turn, 0)
    keep.wait()
    for copy in orders:
        copy.wait()
    spill_order = pltpu.make_async_copy(order_all, order_smem, local_sem.at[10])
    spill_order.start()
    most = pl.ds(0, reps * shards - 1)
    others = pl.ds(0, shards - 1)
    all_asked = copy_to(asked_all.at[most], asked_all.at[most], asked_send, asked_recv, rep, me)
    all_asked.wait()
    spill = pltpu.make_async_copy(asked_all, asked_smem, local_sem.at[11])
    spill.start()
    spill_order.wait()
    spill.wait()

    first_half = lax.broadcasted_iota(I32, (1, 2 * cols), 1) < cols

    def sweep(q, out, got, maps):
        def owner(i, carry):
            peer = peer_at(i)
            slot = lax.rem(i, 2)
            if maps:
                for p in range(2):
                    hist = order_smem[rep, 0, 2 * peer + p]
                    line = asked_all[rep * shards + lax.shift_right_logical(hist, 1)]
                    odd = (hist & 1) == 1
                    maps_out[peer, pl.ds(p, 1), :] = jnp.where(odd, line[1:2], line[0:1])
            for turn_by in range(reps):
                other = lax.rem(rep + turn_by, reps)
                hist = order_smem[other, 0, 2 * peer + q]
                source = other * shards + lax.shift_right_logical(hist, 1)
                odd = hist & 1
                for j in range(half):
                    one = rows[pl.ds(asked_smem[source, odd, j], 1), :]
                    two = rows[pl.ds(asked_smem[source, odd, j + half], 1), :]
                    stage[slot, turn_by, pl.ds(j, 1), :] = jnp.where(first_half, one, two)
                out[other * shards + peer] = stage[slot, turn_by].astype(BF16)

            def send(peer, own):
                for turn_by in range(reps):
                    other = lax.rem(rep + turn_by, reps)

                    def go(other=other):
                        copy_to(
                            out.at[other * shards + peer],
                            got.at[here],
                            row_send.at[q],
                            row_recv.at[q],
                            other,
                            peer,
                        ).start()

                    if turn_by or not own:
                        go()
                if maps and not own:
                    copy_to(
                        maps_out.at[peer], maps_got.at[me], row_send.at[2], row_recv.at[2], rep, peer
                    ).start()

            pl.when(i > 0)(lambda: send(peer_at(i - 1), False))
            pl.when(i == shards - 1)(lambda: send(peer, True))
            return carry

        lax.fori_loop(0, shards, owner, 0)

    sweep(0, soon_out, soon_got, True)
    sweep(1, late_out, late_got, False)
    stays = [
        pltpu.make_async_copy(soon_out.at[here], soon_got.at[here], local_sem.at[12]),
        pltpu.make_async_copy(maps_out.at[me], maps_got.at[me], local_sem.at[13]),
        pltpu.make_async_copy(late_out.at[here], late_got.at[here], local_sem.at[14]),
    ]
    for local in stays:
        local.start()
    soon = copy_to(soon_out.at[most], soon_got.at[most], row_send.at[0], row_recv.at[0], rep, me)
    late = copy_to(late_out.at[most], late_got.at[most], row_send.at[1], row_recv.at[1], rep, me)
    mapped = copy_to(
        maps_out.at[others], maps_got.at[others], row_send.at[2], row_recv.at[2], rep, me
    )
    stays[1].wait()
    mapped.wait_recv()
    kept = [
        pltpu.make_async_copy(maps_got, maps_smem, local_sem.at[15]),
        pltpu.make_async_copy(maps_got, maps_hbm, local_sem.at[16]),
    ]
    for copy in kept:
        copy.start()
    load_proj.wait()
    load_outw.wait()
    kept[0].wait()
    stays[0].wait()
    soon.wait_recv()

    def put(b):
        return store_block(b, mixed_ref, first_hbm, out_sem)

    layer_history(
        0, True, maps_smem, soon_got, proj_ref, outw_ref, put,
        flat, emb, gates, vals, quer, keys, att, mixed_ref,
    )
    for b in range(seq_len // BLOCK):
        put(b).wait()
    kept[1].wait()
    stays[2].wait()
    late.wait_recv()
    for copy in (soon, late, mapped):
        copy.wait_send()


def layer_scratch(seq_len, width, slots):
    head = width // HEADS
    wide = width // 2
    return [
        pltpu.VMEM((2, slots, wide), F32),
        pltpu.VMEM((2, seq_len // 16, 16, wide), F32),
        pltpu.VMEM((seq_len, width), BF16),
        pltpu.VMEM((HEADS, seq_len, head), BF16),
        pltpu.VMEM((HEADS, seq_len, head), BF16),
        pltpu.VMEM((HEADS, seq_len, head), BF16),
        pltpu.VMEM((HEADS, BLOCK, head), F32),
        pltpu.VMEM((seq_len, width), BF16),
        pltpu.SemaphoreType.DMA((seq_len // BLOCK,)),
    ]


def exchange_rows(
    item_ids, lengths, owners, row_home, table, proj_weight, out_weight, shards
):
    cols, rows_dev = table.shape
    seq_dev, seq_len = item_ids.shape
    wide = 2 * cols
    any_space = pl.BlockSpec(memory_space=pl.ANY)
    hbm_space = pl.BlockSpec(memory_space=pltpu.HBM)
    lines = seq_dev * seq_len // 128
    reps = lax.axis_size("rep")
    block = ((reps * shards, CAP // 2, wide), BF16)
    maps = ((shards, seq_dev, 128), I32)
    asked = ((reps * shards, seq_dev, 128), I32)
    order = ((reps, *owners.shape), I32)
    width = proj_weight.shape[0]
    outs = (block, maps, ((seq_len, width), BF16))
    home = row_home.reshape(-1, 128)
    return pl.pallas_call(
        exchange_kernel,
        out_shape=[jax.ShapeDtypeStruct(*shape) for shape in outs],
        in_specs=[hbm_space] * 7,
        out_specs=[any_space] * 3,
        scratch_shapes=[
            pltpu.VMEM(item_ids.shape, I32),
            pltpu.VMEM((lines, 128), I32),
            pltpu.SMEM((lines, 128), I32),
            pltpu.SMEM(lengths.shape, I32),
            pltpu.VMEM(lengths.shape, I32),
            pltpu.VMEM(owners.shape, I32),
            pltpu.VMEM(home.shape, I32),
            pltpu.VMEM((lines, 128, 128), I32),
            pltpu.VMEM(*maps),
            pltpu.VMEM(*asked),
            pltpu.SMEM(*asked),
            pltpu.VMEM(*order),
            pltpu.SMEM(*order),
            pltpu.VMEM((cols, rows_dev), BF16),
            pltpu.VMEM((rows_dev, wide), F32),
            pltpu.VMEM((2, reps, CAP // 2, wide), F32),
            *[pltpu.VMEM(*shape) for shape in (block, block, maps, block, maps)],
            pltpu.SMEM(*maps),
            pltpu.VMEM(proj_weight.shape, BF16),
            pltpu.VMEM(out_weight.shape, BF16),
            *layer_scratch(seq_len, width, shards * CAP),
            pltpu.SemaphoreType.DMA((17,)),
            pltpu.SemaphoreType.DMA,
            pltpu.SemaphoreType.DMA,
            pltpu.SemaphoreType.DMA((reps - 1,)),
            pltpu.SemaphoreType.DMA((reps - 1,)),
            pltpu.SemaphoreType.DMA((3,)),
            pltpu.SemaphoreType.DMA((3,)),
        ],
        compiler_params=pltpu.CompilerParams(
            collective_id=0, has_side_effects=True, vmem_limit_bytes=60 * 1024 * 1024
        ),
        name="exchange",
    )(item_ids, lengths, owners, home, table, proj_weight, out_weight)


def normed_rows(values):
    center = values - jnp.mean(values, axis=-1, keepdims=True)
    spread = jnp.mean(center * center, axis=-1, keepdims=True)
    return center * lax.rsqrt(spread + EPSILON)


def gated_linear(half):
    return half + half * jnp.tanh(half)


def layer_kernel(
    maps_hbm, late_hbm, proj_hbm, outw_hbm, first_hbm, mixed_hbm,
    maps_ref, late_ref, proj_ref, outw_ref, first_ref,
    flat, emb, gates, vals, quer, keys, att, mixed_ref, out_sem, in_sem,
):
    seq_len = mixed_hbm.shape[1]
    loads = [
        pltpu.make_async_copy(source, target, in_sem.at[i])
        for i, (source, target) in enumerate(
            (
                (maps_hbm, maps_ref), (late_hbm, late_ref), (proj_hbm, proj_ref),
                (outw_hbm, outw_ref), (first_hbm, first_ref),
            )
        )
    ]
    for load in loads:
        load.start()
    for load in loads:
        load.wait()
    long_at = jnp.where(maps_ref[0, 0, CAP + 17] > maps_ref[0, 1, CAP + 17], 1, 0)
    move = pltpu.make_async_copy(first_ref, mixed_hbm.at[long_at], in_sem.at[7])
    move.start()

    def put(b):
        return store_block(b, mixed_ref, mixed_hbm.at[1 - long_at], out_sem)

    layer_history(
        1, False, maps_ref, late_ref, proj_ref, outw_ref, put,
        flat, emb, gates, vals, quer, keys, att, mixed_ref, move.wait,
    )
    for b in range(seq_len // BLOCK):
        put(b).wait()


def store_block(b, mixed_ref, mixed_hbm, out_sem):
    span = pl.ds(b * BLOCK, BLOCK)
    return pltpu.make_async_copy(mixed_ref.at[span], mixed_hbm.at[span], out_sem.at[b])


def layer_history(
    seq, whole, maps_ref, got_ref, proj_ref, outw_ref, put,
    flat, emb, gates, vals, quer, keys, att, mixed_ref, ready=None,
):
    seq_len, width = mixed_ref.shape
    head = width // HEADS
    length = maps_ref[0, seq, CAP + 16]
    side = width // 4
    half = got_ref.shape[1]
    shards = got_ref.shape[0] // 4
    group = 8
    first_half = lax.broadcasted_iota(I32, (1, 1, 2 * side), 2) < side

    def place_blocks(c, carry):
        rows = group * 2 * half
        at = pl.multiple_of(c * rows, rows)
        for tile in range(2):
            low, high = (
                got_ref[pl.ds((2 * tile + i) * shards + c * group, group)].astype(F32)
                for i in range(2)
            )
            upper = jnp.where(first_half, low, pltpu.roll(high, side, 2))
            lower = jnp.where(first_half, pltpu.roll(low, side, 2), high)
            flat[tile, pl.ds(at, rows), :] = jnp.concatenate([upper, lower], axis=1).reshape(
                rows, 2 * side
            )
        return carry

    lax.fori_loop(0, shards // group, place_blocks, 0)

    unroll = 16

    def fetch(c, carry):
        for i in range(unroll):
            slot = maps_ref[c, seq, CAP + i]
            for tile in range(2):
                emb[tile, c, pl.ds(i, 1), :] = flat[tile, pl.ds(slot, 1), :]
        return carry

    lax.fori_loop(0, seq_len // unroll if whole else (length + unroll - 1) // unroll, fetch, 0)

    def rows_of(b):
        span = pl.ds(b * (BLOCK // unroll), BLOCK // unroll)
        return jnp.concatenate([emb[t, span].reshape(BLOCK, 2 * side) for t in range(2)], axis=1)

    blocks = seq_len // BLOCK if whole else (length + BLOCK - 1) // BLOCK
    place = lax.broadcasted_iota(I32, (BLOCK, 1), 0)

    def project(b, carry):
        at = pl.multiple_of(b * BLOCK, BLOCK)
        span = pl.ds(at, BLOCK)
        rows = jnp.where(place + at < length, rows_of(b), 0.0)
        normed = normed_rows(rows).astype(BF16)
        for part, ref in enumerate((gates, vals, quer, keys)):
            raw = jnp.dot(
                normed, proj_ref[:, part * width : (part + 1) * width], preferred_element_type=F32
            )
            made = gated_linear(raw * 0.5).astype(BF16)
            if part == 0:
                ref[span, :] = made
            else:
                if part == 2:
                    made = made * (0.5 / math.sqrt(head))
                for h in range(HEADS):
                    ref[h, span, :] = made[:, h * head : (h + 1) * head]
        return carry

    lax.fori_loop(0, blocks, project, 0)
    inverse = 1.0 / length.astype(F32)
    if ready is not None:
        ready()
    keep = lax.broadcasted_iota(I32, (BLOCK, BLOCK), 1) <= lax.broadcasted_iota(
        I32, (BLOCK, BLOCK), 0
    )

    def run(b):
        reach = (b + 1) * BLOCK

        def attend(h, carry):
            query = quer[h, b * BLOCK : reach, :]
            scores = lax.dot_general(
                query, keys[h, :reach, :], (((1,), (1,)), ((), ())), preferred_element_type=F32
            )
            weights = gated_linear(scores)
            last = jnp.where(keep, weights[:, b * BLOCK :], 0.0).astype(BF16)
            if b:
                last = jnp.concatenate([weights[:, : b * BLOCK].astype(BF16), last], axis=1)
            att[h] = jnp.dot(last, vals[h, :reach, :], preferred_element_type=F32)
            return carry

        lax.fori_loop(0, HEADS, attend, 0)
        joined = jnp.concatenate([att[h] for h in range(HEADS)], axis=1) * inverse
        gated = (normed_rows(joined) * gates[b * BLOCK : reach, :].astype(F32)).astype(BF16)
        mixed = rows_of(b) + jnp.dot(gated, outw_ref[...], preferred_element_type=F32)
        live = place + b * BLOCK < length
        mixed_ref[b * BLOCK : reach, :] = jnp.where(live, mixed, 0.0).astype(BF16)

    for b in range(seq_len // BLOCK):
        if whole:
            run(b)
        else:
            pl.when(b * BLOCK < length)(lambda b=b: run(b))

            @pl.when(b * BLOCK >= length)
            def _(b=b):
                mixed_ref[b * BLOCK : (b + 1) * BLOCK, :] = jnp.zeros((BLOCK, width), BF16)

        put(b).start()


def layer(maps, late, first, proj_weight, out_weight):
    slots = maps.shape[0] * CAP
    seq_len, width = first.shape
    return pl.pallas_call(
        layer_kernel,
        out_shape=jax.ShapeDtypeStruct((maps.shape[1], seq_len, width), BF16),
        in_specs=[pl.BlockSpec(memory_space=pltpu.HBM)] * 5,
        out_specs=pl.BlockSpec(memory_space=pltpu.HBM),
        scratch_shapes=[
            pltpu.SMEM(maps.shape, I32),
            pltpu.VMEM(late.shape, BF16),
            pltpu.VMEM(proj_weight.shape, BF16),
            pltpu.VMEM(out_weight.shape, BF16),
            pltpu.VMEM(first.shape, BF16),
            *layer_scratch(seq_len, width, slots),
            pltpu.SemaphoreType.DMA((8,)),
        ],
        compiler_params=pltpu.CompilerParams(vmem_limit_bytes=60 * 1024 * 1024),
        name="layer",
    )(maps, late, proj_weight, out_weight, first)


def body(item_ids, seq_lengths, seq_owner, row_home, item_table, proj_weight, out_weight):
    shards = lax.axis_size("shard")
    late, maps, first = exchange_rows(
        item_ids, seq_lengths, seq_owner, row_home, item_table.T, proj_weight, out_weight, shards
    )
    return layer(maps, late, first, proj_weight, out_weight)


def solution(mesh):
    in_specs = (
        P(("rep", "shard"), None),
        P("rep", None),
        P("rep", None),
        P(),
        P("shard", "rep"),
        P(),
        P(),
    )
    out_specs = P(("rep", "shard"), None, None)
    return jax.shard_map(body, mesh=mesh, in_specs=in_specs, out_specs=out_specs, check_vma=False)
```

time: 96.2 us -> 93.1 us (0.968)
  Pallas kernels: 95.1 us -> 92.2 us
    pallas_call x1, Pallas kernels: 88.7 us -> 86 us  [exchange_rows(): pl.pallas_call(exchange_kernel, out_shape=[jax.ShapeDtypeStruct(*shape) f...]
where the time goes in v6:
time: 93.1 us; the launch traced here: 92.2 us
  Pallas kernels  92.2 us (99%)
    pallas_call x1, Pallas kernels, exchange_rows(): pl.pallas_call(exchange_kernel, out_shape=[jax.ShapeDtypeStruct(*shape) f...  86 us
    pallas_call x1, Pallas kernels, layer(): pl.pallas_call(layer_kernel, out_shape=jax.ShapeDtypeStruct((maps.shape[1...  6.19 us

profile of v6, /device:TPU:1, one launch (start us, length us, event | category | flops | bytes accessed | tf_op | source)
XLA Modules:
  0.0 92.2 jit_solution(9362296037668338256)
XLA Ops:
  0.0 86.0 %exchange.1 = (bf16[256,16,128]{2,1,0:T(8,128)(2,1)}, s32[64,2,128]{2,1,0:T(2,128)}, bf16[1024,256]{1,0:T(8,128)(2,1)}) custom-call(s32[2,1024]{1,0:T(2,128)} %ids_hbm.1, s32[1,128]{1,0:T(1,128)} %len_hbm.1, s32[1,128]{1,0:T(1,128)} %owner_hbm.1, s32[4096,128]{1,0:T(8,128)} %bitcast.2, bf16[64,8192]{1,0:T(8,128)(2,1)} %bitcast.3, ...), custom_call_target="tpu_custom_call" | custom-call | tf_op jit(solution)/shard_map/exchange/pallas_call | solution.py:395
  86.0 6.2 %layer.1 = bf16[2,1024,256]{2,1,0:T(8,128)(2,1)} custom-call(s32[64,2,128]{2,1,0:T(2,128)} %get-tuple-element.8.maps_hbm, bf16[256,16,128]{2,1,0:T(8,128)(2,1)} %get-tuple-element.9.late_hbm, bf16[256,1024]{1,0:T(8,128)(2,1)} %proj_hbm.3, bf16[256,256]{1,0:T(8,128)(2,1)} %outw_hbm.3, bf16[1024,256]{1,0:T(8,128)(2,1)} %get-tuple-element.10.first_hbm), custom_call_target="tpu_custom_call" | custom-call | tf_op jit(solution)/shard_map/layer/pallas_call | solution.py:599

commit v7 on v6

--- a/solution.py
+++ b/solution.py
@@ -50,8 +50,7 @@
 def plan_fetch(ids_smem, home, stage):
     def fetch(c, carry):
         for i in range(128):
-            line = lax.shift_right_logical(ids_smem[c, i], 7)
-            stage[c, pl.ds(i, 1), :] = home[pl.ds(line, 1), :]
+            stage[c, pl.ds(i, 1), :] = home[pl.ds(ids_smem[c, i], 1), :]
         return carry
 
     lax.fori_loop(0, ids_smem.shape[0], fetch, 0)
@@ -110,7 +109,7 @@
     ids_hbm, len_hbm, owner_hbm, home_ref, table_ref, proj_hbm, outw_hbm,
     late_got, maps_hbm, first_hbm,
     ids_ref, ids_lines, ids_smem, len_smem, len_ref, owner_ref, home_in, lines,
-    asked_ref, asked_all, asked_smem, order_all, order_smem, table_in, rows, stage,
+    asked_ref, asked_all, asked_two, asked_smem, order_all, order_smem, table_in, rows, stage,
     soon_out, late_out, maps_out, soon_got, maps_got, maps_smem, proj_ref, outw_ref,
     flat, emb, gates, vals, quer, keys, att, mixed_ref, out_sem, local_sem,
     asked_send, asked_recv, order_send, order_recv, row_send, row_recv,
@@ -145,28 +144,35 @@
     spread = shards // (2 * depth)
 
     def toward(i, size):
-        step = (i + 1) // 2
+        step = lax.div(i + 1, 2)
         return lax.rem(size // 2 + step * (2 * lax.rem(i, 2) - 1) + size, size)
 
     def peer_at(i):
-        dz = toward(i // (2 * spread), depth)
-        dx = toward(lax.rem(i // 2, spread), spread)
+        dz = toward(lax.div(i, 2 * spread), depth)
+        dx = toward(lax.rem(lax.div(i, 2), spread), spread)
         core = lax.rem(lax.rem(me, 2) + 1 + lax.rem(i, 2), 2)
-        z = lax.rem(me // 2 + dz, depth)
-        x = lax.rem(me // (2 * depth) + dx, spread)
+        z = lax.rem(lax.div(me, 2) + dz, depth)
+        x = lax.rem(lax.div(me, 2 * depth) + dx, spread)
         return (x * depth + z) * 2 + core
 
     def greet(i, carry):
-        other = lax.rem(here + i, reps * shards)
-        pl.semaphore_signal(
-            barrier,
-            inc=1,
-            device_id={"rep": other // shards, "shard": lax.rem(other, shards)},
-            device_id_type=pl.DeviceIdType.MESH,
-        )
+        peer = lax.rem(me + i, shards)
+        for turn_by in range(reps):
+            def go(turn_by=turn_by):
+                pl.semaphore_signal(
+                    barrier,
+                    inc=1,
+                    device_id={"rep": lax.rem(rep + turn_by, reps), "shard": peer},
+                    device_id_type=pl.DeviceIdType.MESH,
+                )
+
+            if turn_by == 0:
+                pl.when(i < shards)(go)
+            else:
+                go()
         return carry
 
-    lax.fori_loop(1, reps * shards, greet, 0)
+    lax.fori_loop(1, shards + 1, greet, 0)
 
     eye = (
         lax.broadcasted_iota(I32, (chunk, chunk), 0) == lax.broadcasted_iota(I32, (chunk, chunk), 1)
@@ -187,7 +193,9 @@
     for seq in range(seq_dev):
         for b in range(seq_len // 128):
             at = seq * (seq_len // 128) + b
-            ids_lines[at : at + 1, :] = ids_ref[seq : seq + 1, b * 128 : (b + 1) * 128]
+            ids_lines[at : at + 1, :] = lax.shift_right_logical(
+                ids_ref[seq : seq + 1, b * 128 : (b + 1) * 128], 7
+            ) & (home_in.shape[0] - 1)
     spill_ids = pltpu.make_async_copy(ids_lines, ids_smem, local_sem.at[8])
     spill_ids.start()
     load_owner.wait()
@@ -197,12 +205,12 @@
     load_home.wait()
     plan_fetch(ids_smem, home_in, lines)
     load_len.wait()
+    parts = []
     for seq in range(seq_dev):
         index = me * seq_dev + seq
         length = len_smem[0, index]
-        asked_ref[:, seq, :] = plan_requests(
-            seq, length, index, ids_ref, lines, shards, rows_dev
-        )
+        parts.append(plan_requests(seq, length, index, ids_ref, lines, shards, rows_dev))
+    asked_ref[...] = (parts[0] + pltpu.roll(parts[1], 64, 1)).reshape(asked_ref.shape)
     load.wait()
     load_proj.start()
     load_outw.start()
@@ -260,7 +268,11 @@
     others = pl.ds(0, shards - 1)
     all_asked = copy_to(asked_all.at[most], asked_all.at[most], asked_send, asked_recv, rep, me)
     all_asked.wait()
-    spill = pltpu.make_async_copy(asked_all, asked_smem, local_sem.at[11])
+    both = asked_all[...].reshape(reps * shards, 128)
+    at_row = lax.broadcasted_iota(I32, both.shape, 1) < CAP
+    for q, line in enumerate((both, pltpu.roll(both, 64, 1))):
+        asked_two[q] = jnp.where(at_row, line & (rows_dev - 1), line & (shards * CAP - 1))
+    spill = pltpu.make_async_copy(asked_two, asked_smem, local_sem.at[11])
     spill.start()
     spill_order.wait()
     spill.wait()
@@ -274,17 +286,16 @@
             if maps:
                 for p in range(2):
                     hist = order_smem[rep, 0, 2 * peer + p]
-                    line = asked_all[rep * shards + lax.shift_right_logical(hist, 1)]
-                    odd = (hist & 1) == 1
-                    maps_out[peer, pl.ds(p, 1), :] = jnp.where(odd, line[1:2], line[0:1])
+                    at = rep * shards + lax.shift_right_logical(hist, 1)
+                    maps_out[peer, pl.ds(p, 1), :] = asked_two[hist & 1, pl.ds(at, 1), :]
             for turn_by in range(reps):
                 other = lax.rem(rep + turn_by, reps)
                 hist = order_smem[other, 0, 2 * peer + q]
                 source = other * shards + lax.shift_right_logical(hist, 1)
                 odd = hist & 1
                 for j in range(half):
-                    one = rows[pl.ds(asked_smem[source, odd, j], 1), :]
-                    two = rows[pl.ds(asked_smem[source, odd, j + half], 1), :]
+                    one = rows[pl.ds(asked_smem[odd, source, j], 1), :]
+                    two = rows[pl.ds(asked_smem[odd, source, j + half], 1), :]
                     stage[slot, turn_by, pl.ds(j, 1), :] = jnp.where(first_half, one, two)
                 out[other * shards + peer] = stage[slot, turn_by].astype(BF16)
 
@@ -387,7 +398,7 @@
     reps = lax.axis_size("rep")
     block = ((reps * shards, CAP // 2, wide), BF16)
     maps = ((shards, seq_dev, 128), I32)
-    asked = ((reps * shards, seq_dev, 128), I32)
+    asked = ((seq_dev, reps * shards, 128), I32)
     order = ((reps, *owners.shape), I32)
     width = proj_weight.shape[0]
     outs = (block, maps, ((seq_len, width), BF16))
@@ -406,7 +417,8 @@
             pltpu.VMEM(owners.shape, I32),
             pltpu.VMEM(home.shape, I32),
             pltpu.VMEM((lines, 128, 128), I32),
-            pltpu.VMEM(*maps),
+            pltpu.VMEM((shards, 1, 128), I32),
+            pltpu.VMEM((reps * shards, 1, 128), I32),
             pltpu.VMEM(*asked),
             pltpu.SMEM(*asked),
             pltpu.VMEM(*order),
@@ -461,18 +473,22 @@
     ]
     for load in loads:
         load.start()
-    for load in loads:
+    for load in loads[:2]:
         load.wait()
     long_at = jnp.where(maps_ref[0, 0, CAP + 17] > maps_ref[0, 1, CAP + 17], 1, 0)
     move = pltpu.make_async_copy(first_ref, mixed_hbm.at[long_at], in_sem.at[7])
-    move.start()
+
+    def weights():
+        for load in loads[2:]:
+            load.wait()
+        move.start()
 
     def put(b):
         return store_block(b, mixed_ref, mixed_hbm.at[1 - long_at], out_sem)
 
     layer_history(
         1, False, maps_ref, late_ref, proj_ref, outw_ref, put,
-        flat, emb, gates, vals, quer, keys, att, mixed_ref, move.wait,
+        flat, emb, gates, vals, quer, keys, att, mixed_ref, weights, move.wait,
     )
     for b in range(seq_len // BLOCK):
         put(b).wait()
@@ -485,7 +501,7 @@
 
 def layer_history(
     seq, whole, maps_ref, got_ref, proj_ref, outw_ref, put,
-    flat, emb, gates, vals, quer, keys, att, mixed_ref, ready=None,
+    flat, emb, gates, vals, quer, keys, att, mixed_ref, weights=None, ready=None,
 ):
     seq_len, width = mixed_ref.shape
     head = width // HEADS
@@ -550,6 +566,8 @@
                     ref[h, span, :] = made[:, h * head : (h + 1) * head]
         return carry
 
+    if weights is not None:
+        weights()
     lax.fori_loop(0, blocks, project, 0)
     inverse = 1.0 / length.astype(F32)
     if ready is not None:

time: 93.1 us -> 89.4 us (0.960)
  Pallas kernels: 92.2 us -> 88.5 us
    pallas_call x1, Pallas kernels: 86 us -> 82.3 us  [exchange_rows(): pl.pallas_call(exchange_kernel, out_shape=[jax.ShapeDtypeStruct(*shape) f...]
where the time goes in v7:
time: 89.4 us; the launch traced here: 88.6 us
  Pallas kernels  88.5 us (99%)
    pallas_call x1, Pallas kernels, exchange_rows(): pl.pallas_call(exchange_kernel, out_shape=[jax.ShapeDtypeStruct(*shape) f...  82.3 us
    pallas_call x1, Pallas kernels, layer(): pl.pallas_call(layer_kernel, out_shape=jax.ShapeDtypeStruct((maps.shape[1...  6.2 us

profile of v7, /device:TPU:1, one launch (start us, length us, event | category | flops | bytes accessed | tf_op | source)
XLA Modules:
  0.0 88.6 jit_solution(10929394657754757608)
XLA Ops:
  0.0 82.3 %exchange.1 = (bf16[256,16,128]{2,1,0:T(8,128)(2,1)}, s32[64,2,128]{2,1,0:T(2,128)}, bf16[1024,256]{1,0:T(8,128)(2,1)}) custom-call(s32[2,1024]{1,0:T(2,128)} %ids_hbm.1, s32[1,128]{1,0:T(1,128)} %len_hbm.1, s32[1,128]{1,0:T(1,128)} %owner_hbm.1, s32[4096,128]{1,0:T(8,128)} %bitcast.2, bf16[64,8192]{1,0:T(8,128)(2,1)} %bitcast.3, ...), custom_call_target="tpu_custom_call" | custom-call | tf_op jit(solution)/shard_map/exchange/pallas_call | solution.py:406
  82.4 6.2 %layer.1 = bf16[2,1024,256]{2,1,0:T(8,128)(2,1)} custom-call(s32[64,2,128]{2,1,0:T(2,128)} %get-tuple-element.8.maps_hbm, bf16[256,16,128]{2,1,0:T(8,128)(2,1)} %get-tuple-element.9.late_hbm, bf16[256,1024]{1,0:T(8,128)(2,1)} %proj_hbm.3, bf16[256,256]{1,0:T(8,128)(2,1)} %outw_hbm.3, bf16[1024,256]{1,0:T(8,128)(2,1)} %get-tuple-element.10.first_hbm), custom_call_target="tpu_custom_call" | custom-call | tf_op jit(solution)/shard_map/layer/pallas_call | solution.py:617
